TPU v7x, 256 devices: a whole 4x4x8 slice. The times are simulated.
256 devices in a mesh: segment: 4 (over x), amp: 64 (over y, z, core).
Axes of the slice: x: 4, y: 4, z: 8, core: 2. Of those that a mesh axis runs over, the one named last changes fastest.
Arguments:
- states: float32 [4, 16777216], P('segment', 'amp'), may hold values from -6 to 6
- gate_blocks: float32 [4, 3, 128, 128], P('segment'), may hold values from -1 to 1, as said below
- kraus_picks: int32 [4, 4, 3, 7], P('segment'), may hold values from 0 to 3
- block_targets: int32 [4, 3], replicated, may hold values from 0 to 1
Outputs:
- final_states: float32 [4, 16777216], P('segment', 'amp')
- log_weights: float32 [4, 4], P('segment')
Inputs may be any that keep to these rules, and one draw needn't show every extreme that they name: Every block of gate_blocks is an orthogonal matrix, up to rounding.
All inputs are finite; a program needn't handle non-finite values.
Results may differ from a plain program's by a relative error of at most 0.0003.
Values sent between devices are 32-bit elements; how exact they have to be, the bound alone decides.
A program may use at most 64 MiB of HBM per device.

v0:
```python
import functools

import jax
import jax.numpy as jnp
from jax import lax
from jax.experimental import pallas as pl
from jax.experimental.pallas import tpu as pltpu
from jax.sharding import PartitionSpec as P

KEEP_FACTORS = (1.0, 0.9, 1.0, 0.97)
FLIP_FACTORS = (0.9, 1.0, 0.97, 1.0)
QUBITS = 7
REG = 128
MID = 16
PEERS = 64
SECTIONS = 4
BLOCKS = 3
ROWS = 2048
MESH = pl.DeviceIdType.MESH
F32 = jnp.float32
BF16 = jnp.bfloat16


def split(x):
    hi = x.astype(BF16)
    lo = (x - hi.astype(F32)).astype(BF16)
    return hi, lo


def exact_dot(a, b):
    return jnp.dot(a, b, precision=lax.Precision.HIGHEST, preferred_element_type=F32)


def mix_rows(gate_cat, x):
    hi, lo = split(x)
    return jnp.dot(gate_cat, jnp.concatenate([hi, hi, lo], axis=0), preferred_element_type=F32)


def mix_lanes(x, gate_cat):
    hi, lo = split(x)
    return jnp.dot(jnp.concatenate([hi, hi, lo], axis=1), gate_cat, preferred_element_type=F32)


def rows_cat(gate):
    hi, lo = split(gate)
    return jnp.concatenate([hi, lo, hi], axis=1)


def lanes_cat(gate_t):
    hi, lo = split(gate_t)
    return jnp.concatenate([hi, lo, hi], axis=0)


def block_transpose(arrays):
    lane = lax.broadcasted_iota(jnp.int32, arrays[0].shape, 1)
    low_half = lane < 64
    even = (lane // 32) % 2 == 0
    stage = [None] * 4
    for a in range(2):
        moved = pltpu.roll(jnp.where(low_half, arrays[a + 2], arrays[a]), 64, 1)
        stage[a] = jnp.where(low_half, arrays[a], moved)
        stage[a + 2] = jnp.where(low_half, moved, arrays[a + 2])
    result = [None] * 4
    for a in (0, 2):
        result[a] = jnp.where(even, stage[a], pltpu.roll(stage[a + 1], 32, 1))
        result[a + 1] = jnp.where(even, pltpu.roll(stage[a], 96, 1), stage[a + 1])
    return result


def fold_squares(acc, x):
    sq = x * x
    return acc + jnp.sum(sq.reshape(sq.shape[0] // 8, 8, sq.shape[1]), axis=0)


def amp_of(m, j):
    return (m // 8) * 32 + (j // 2) * 16 + (m % 8) * 2 + j % 2


def scalar_pick(kind, table):
    return jnp.where(
        kind == 0,
        F32(table[0]),
        jnp.where(kind == 1, F32(table[1]), jnp.where(kind == 2, F32(table[2]), F32(table[3]))),
    )


def kernel(
    x_ref, gate_ref, kraus_ref, target_ref,
    y_ref, stats_ref,
    all_gates, send1, recv1, mid2, mid3, half2, recv2, send3, recv3, h_mats, l01_mat, l2_mat, l23_mat, sums_out, sums_in,
    gate_send, gate_recv, pair_send, pair_recv,
    send1_sem, recv1_sem, send2_sem, recv2_sem, send3_sem, recv3_sem, sums_send, sums_recv,
):
    seg = lax.axis_index("segment")
    me = lax.axis_index("amp")
    y_pos = me // 16
    j_me = (y_pos % 2) * 2 + me % 2
    m_me = (y_pos // 2) * 8 + (me % 16) // 2
    core = me % 2
    partner = me + 1 - 2 * core
    zero = jnp.zeros((8, REG), F32)

    def at(ref, index, rows):
        return ref.at[pl.ds(pl.multiple_of(index * rows, rows), rows)]

    barrier = pltpu.get_barrier_semaphore()

    def greet(k, carry):
        pl.semaphore_signal(barrier, inc=1, device_id=(seg, (me + k) % PEERS), device_id_type=MESH)
        return carry

    lax.fori_loop(1, PEERS, greet, 0)
    for k in range(1, SECTIONS):
        pl.semaphore_signal(barrier, inc=1, device_id=((seg + k) % SECTIONS, me), device_id_type=MESH)

    all_gates[seg] = gate_ref[...]

    pl.semaphore_wait(barrier, PEERS - 1 + SECTIONS - 1)

    my_half = pl.ds(pl.multiple_of(core * 64, 64), 64)
    other_half = pl.ds(pl.multiple_of((1 - core) * 64, 64), 64)

    def gate_copy(section, target_seg):
        return pltpu.make_async_remote_copy(
            gate_ref.at[:, my_half, :],
            all_gates.at[section, :, my_half, :],
            gate_send.at[target_seg],
            gate_recv.at[section],
            device_id=(target_seg, me),
            device_id_type=MESH,
        )

    def pair_copy(section):
        return pltpu.make_async_remote_copy(
            all_gates.at[section, :, my_half, :],
            all_gates.at[section, :, my_half, :],
            pair_send.at[section],
            pair_recv.at[section],
            device_id=(seg, partner),
            device_id_type=MESH,
        )

    def send_gates(section):
        @pl.when(seg == section)
        def _():
            for k in range(1, SECTIONS):
                gate_copy(section, (seg + k) % SECTIONS).start()

    def pass_gates(section):
        @pl.when(seg != section)
        def _():
            gate_copy(section, section).wait_recv()
            pair_copy(section).start()

    def end_gates(section):
        @pl.when(seg != section)
        def _():
            pltpu.make_async_copy(
                all_gates.at[section, :, other_half, :], all_gates.at[section, :, other_half, :], pair_recv.at[section]
            ).wait()

    row = lax.broadcasted_iota(jnp.int32, (REG, REG), 0)
    col = lax.broadcasted_iota(jnp.int32, (REG, REG), 1)
    identity = (row == col).astype(F32)
    to_split = (col == (row % 64) * 2 + row // 64).astype(F32)
    from_split = (row == (col % 64) * 2 + col // 64).astype(F32)

    def noise(section, block):
        product = jnp.ones((REG, REG), F32)
        for q in range(QUBITS):
            kind = kraus_ref[section, block, q]
            bit = lax.shift_right_logical(row, QUBITS - 1 - q) & 1
            product = product * jnp.where(bit == 1, scalar_pick(kind, FLIP_FACTORS), scalar_pick(kind, KEEP_FACTORS))
        return product

    def compose(section):
        low, high = identity, identity
        for block in range(BLOCKS):
            on_low = target_ref[section, block] == 0
            gate = all_gates[section, block]
            if block == 0:
                mixed = gate
            else:
                mixed = exact_dot(gate, jnp.where(on_low, low, high))
            mixed = noise(section, block) * mixed
            low, high = jnp.where(on_low, mixed, low), jnp.where(on_low, high, mixed)
        return low, high

    send_gates(0)
    send_gates(1)
    pass_gates(0)
    pass_gates(1)
    end_gates(0)
    low0, high0 = compose(0)
    h_mats[0] = rows_cat(high0)
    end_gates(1)
    low1, high1 = compose(1)
    h_mats[1] = rows_cat(exact_dot(high1, from_split))
    l01_mat[...] = jnp.concatenate([lanes_cat(low0.T), lanes_cat(exact_dot(low1, low0).T)], axis=1)

    width = 2

    def send_piece1(m, j):
        to = amp_of(m, j)

        @pl.when(to != me)
        def _():
            pltpu.make_async_remote_copy(
                at(send1, m * 4 + j, 32), at(recv1, me, 32), send1_sem, recv1_sem, device_id=(seg, to), device_id_type=MESH
            ).start()

    def send_chunk1(k):
        def one(n, carry):
            send_piece1((m_me + k * width + n // 4) % MID, (j_me + n) % 4)
            return carry

        lax.fori_loop(0, 4 * width, one, 0)

    def section0(k, sums):
        first, after = sums
        ms = [(m_me + k * width + i) % MID for i in range(width)]
        xs = [x_ref[pl.ds(m, REG, stride=MID), :] for m in ms]
        for x in xs:
            first = fold_squares(first, x)
        wide = mix_rows(h_mats[0], jnp.concatenate(xs, axis=1))
        tall = jnp.concatenate([wide[:, i * REG : (i + 1) * REG] for i in range(width)], axis=0)
        both = mix_lanes(tall, l01_mat[...])
        after = fold_squares(after, both[:, :REG])
        for i, m in enumerate(ms):
            pieces = block_transpose([both[i * REG + q * 32 : i * REG + (q + 1) * 32, REG:] for q in range(4)])
            for j in range(4):
                send1[pl.ds(pl.multiple_of((m * 4 + j) * 32, 32), 32), :] = pieces[j]

        @pl.when(k > 0)
        def _():
            send_chunk1(k - 1)

        return first, after

    first_sum, sum0 = lax.fori_loop(0, MID // width, section0, (zero, zero))
    send_chunk1(MID // width - 1)
    recv1[pl.ds(pl.multiple_of(me * 32, 32), 32), :] = send1[pl.ds(pl.multiple_of((m_me * 4 + j_me) * 32, 32), 32), :]

    send_gates(2)
    send_gates(3)
    pass_gates(2)
    pass_gates(3)
    end_gates(2)
    low2, high2 = compose(2)
    h_mats[2] = rows_cat(exact_dot(high2, from_split))
    l2_mat[...] = lanes_cat(low2.T)
    end_gates(3)
    low3, high3 = compose(3)
    h_mats[3] = rows_cat(exact_dot(to_split, exact_dot(high3, from_split)))
    l23_mat[...] = lanes_cat(exact_dot(low3, low2).T)

    def wait_bytes(ref, rows, sem):
        pltpu.make_async_copy(ref.at[pl.ds(0, rows)], ref.at[pl.ds(0, rows)], sem).wait()

    def split_rows(ref, index):
        return jnp.concatenate(
            [ref[pl.ds(2 * index, 64, stride=32), :], ref[pl.ds(2 * index + 1, 64, stride=32), :]], axis=0
        )

    wait_bytes(recv1, 63 * 32, recv1_sem)

    step = 4

    def section1(k, acc):
        rs = [k * step + i for i in range(step)]
        wide = mix_rows(h_mats[1], jnp.concatenate([split_rows(recv1, r) for r in rs], axis=1))
        acc = fold_squares(acc, wide[:, :REG])
        for i in range(1, step):
            acc = fold_squares(acc, wide[:, i * REG : (i + 1) * REG])
        for i, r in enumerate(rs):
            parts = block_transpose([wide[q * 32 : (q + 1) * 32, i * REG : (i + 1) * REG] for q in range(4)])
            for q in range(4):
                mid2[pl.ds(pl.multiple_of((q * 16 + r) * 32, 32), 32), :] = parts[q]
        return acc

    sum1 = lax.fori_loop(0, 16 // step, section1, zero)

    def section2(k, carry):
        ks = [k * step + i for i in range(step)]
        wide = mix_rows(h_mats[2], jnp.concatenate([split_rows(mid2, r) for r in ks], axis=1))
        for i, r in enumerate(ks):
            here = wide[:, i * REG : (i + 1) * REG]
            half2[pl.ds(pl.multiple_of(r * REG, REG), REG), :] = here
            parts = block_transpose([here[q * 32 : (q + 1) * 32] for q in range(4)])
            for q in range(4):
                mid3[pl.ds(pl.multiple_of((q * 16 + r) * 32, 32), 32), :] = parts[q]
        return carry

    lax.fori_loop(0, 16 // step, section2, 0)

    def send_half2(k, carry):
        j = (j_me + k) % 4
        pltpu.make_async_remote_copy(
            at(half2, j, 512), at(recv2, j_me, 512), send2_sem, recv2_sem,
            device_id=(seg, amp_of(m_me, j)), device_id_type=MESH,
        ).start()
        return carry

    lax.fori_loop(1, 4, send_half2, 0)

    def section3(k, carry):
        rs = [k * step + i for i in range(step)]
        wide = mix_rows(h_mats[3], jnp.concatenate([split_rows(mid3, r) for r in rs], axis=1))
        for i, r in enumerate(rs):
            here = wide[:, i * REG : (i + 1) * REG]
            send3[pl.ds(2 * r, 64, stride=32), :] = here[:64]
            send3[pl.ds(2 * r + 1, 64, stride=32), :] = here[64:]
        return carry

    lax.fori_loop(0, 16 // step, section3, 0)
    slot = m_me * 4 + j_me

    def send_piece3(k, carry):
        to = (me + k) % PEERS
        pltpu.make_async_remote_copy(
            at(send3, to, 32), at(recv3, slot, 32), send3_sem, recv3_sem, device_id=(seg, to), device_id_type=MESH
        ).start()
        return carry

    lax.fori_loop(1, PEERS, send_piece3, 0)
    recv3[pl.ds(pl.multiple_of(slot * 32, 32), 32), :] = send3[pl.ds(pl.multiple_of(me * 32, 32), 32), :]

    own = pl.ds(pl.multiple_of(j_me * 512, 512), 512)
    wait_bytes(recv2, 3 * 512, recv2_sem)
    recv2[own, :] = half2[own, :]

    def norm2(k, acc):
        parts = block_transpose(
            [recv2[pl.ds(pl.multiple_of(j * 512 + k * REG, REG), REG), :] for j in range(4)]
        )
        return fold_squares(acc, mix_lanes(jnp.concatenate(parts, axis=0), l2_mat[...]))

    sum2 = lax.fori_loop(0, 4, norm2, zero)
    wait_bytes(recv3, 63 * 32, recv3_sem)

    def last(k, acc):
        ms = [k * step + i for i in range(step)]
        tall = []
        for m in ms:
            tall += block_transpose([recv3[pl.ds(pl.multiple_of((m * 4 + j) * 32, 32), 32), :] for j in range(4)])
        mixed = mix_lanes(jnp.concatenate(tall, axis=0), l23_mat[...])
        for i, m in enumerate(ms):
            y_ref[pl.ds(m, REG, stride=MID), :] = mixed[i * REG : (i + 1) * REG]
        return fold_squares(acc, mixed)

    sum3 = lax.fori_loop(0, MID // step, last, zero)

    lane = lax.broadcasted_iota(jnp.int32, (1, REG), 1)
    line = jnp.zeros((1, REG), F32)
    for n, acc in enumerate((first_sum, sum0, sum1, sum2, sum3)):
        line = jnp.where(lane == n, jnp.sum(acc), line)
    sums_out[...] = line
    sums_in[me] = line

    def send_sums(k, carry):
        to = (me + k) % PEERS
        pltpu.make_async_remote_copy(
            sums_out, sums_in.at[me], sums_send, sums_recv, device_id=(seg, to), device_id_type=MESH
        ).start()
        return carry

    lax.fori_loop(1, PEERS, send_sums, 0)

    for section in range(SECTIONS):
        @pl.when(seg == section)
        def _():
            for k in range(1, SECTIONS):
                gate_copy(section, (seg + k) % SECTIONS).wait_send()

        @pl.when(seg != section)
        def _():
            pair_copy(section).wait_send()

    wait_bytes(send1, 63 * 32, send1_sem)
    wait_bytes(half2, 3 * 512, send2_sem)
    wait_bytes(send3, 63 * 32, send3_sem)
    wait_bytes(sums_in, 63, sums_send)
    wait_bytes(sums_in, 63, sums_recv)
    stats_ref[...] = jnp.sum(sums_in[...], axis=0)


def body(states, gate_blocks, kraus_picks, block_targets):
    amp_local = states.shape[1]
    total_amps = amp_local * lax.axis_size("amp")
    dma = pltpu.SemaphoreType.DMA
    vmem = pl.BlockSpec(memory_space=pltpu.VMEM)
    smem = pl.BlockSpec(memory_space=pltpu.SMEM)
    big = pltpu.VMEM((ROWS, REG), F32)
    values, totals = pl.pallas_call(
        kernel,
        out_shape=(jax.ShapeDtypeStruct((ROWS, REG), F32), jax.ShapeDtypeStruct((1, REG), F32)),
        in_specs=[vmem, vmem, smem, smem],
        out_specs=(vmem, vmem),
        scratch_shapes=[
            pltpu.VMEM((SECTIONS, BLOCKS, REG, REG), F32),
            big, big, big, big, big, big, big, big,
            pltpu.VMEM((SECTIONS, REG, 3 * REG), BF16),
            pltpu.VMEM((3 * REG, 2 * REG), BF16),
            pltpu.VMEM((3 * REG, REG), BF16),
            pltpu.VMEM((3 * REG, REG), BF16),
            pltpu.VMEM((1, REG), F32),
            pltpu.VMEM((PEERS, 1, REG), F32),
            dma((SECTIONS,)), dma((SECTIONS,)), dma((SECTIONS,)), dma((SECTIONS,)),
            dma, dma, dma, dma, dma, dma, dma, dma,
        ],
        compiler_params=pltpu.CompilerParams(collective_id=0, has_side_effects=True),
        name="trajectory",
    )(states.reshape(ROWS, REG), gate_blocks[0], kraus_picks[0], block_targets)
    totals = totals[0]
    log_weights = jnp.log(totals[1:5] / totals[0:4])
    scaled = values / jnp.sqrt(totals[4] / total_amps)
    return scaled.reshape(1, amp_local), log_weights.reshape(1, SECTIONS)


def solution(mesh):
    in_specs = (
        P("segment", "amp"),
        P("segment", None, None, None),
        P("segment", None, None, None),
        P(),
    )
    out_specs = (P("segment", "amp"), P("segment", None))
    return jax.shard_map(body, mesh=mesh, in_specs=in_specs, out_specs=out_specs, check_vma=False)
```

profile of v0, /device:TPU:1, one launch (start us, length us, event | category | flops | bytes accessed | tf_op | source)
XLA Modules:
  0.0 96.8 jit_solution(14710880079947913622)
XLA Ops:
  0.6 1.3 %copy.6.kraus_ref = s32[4,3,7]{2,1,0:T(4,128)} copy(s32[4,3,7]{2,0,1:T(4,128)} %bitcast.8) | data formatting | bytes 672 | tf_op jit(solution)/shard_map/squeeze | solution.py:413
  1.9 90.1 %trajectory.1 = (f32[2048,128]{1,0:T(8,128)}, f32[1,128]{1,0:T(1,128)}) custom-call(f32[2048,128]{1,0:T(8,128)} %bitcast.6, f32[3,128,128]{2,1,0:T(8,128)} %bitcast.7, s32[4,3,7]{2,1,0:T(4,128)} %copy.6.kraus_ref, s32[4,3]{1,0:T(4,128)} %target_ref.1), custom_call_target="tpu_custom_call" | custom-call | tf_op jit(solution)/shard_map/trajectory/pallas_call | solution.py:394
  92.0 0.0 copy-start
  92.1 0.6 copy-done
  92.7 0.6 slice.12
  93.9 2.3 %broadcast_divide_fusion = f32[2048,128]{1,0:T(8,128)} fusion(f32[2048,128]{1,0:T(8,128)} %get-tuple-element.4, f32[]{:T(128)} %bitcast.3), kind=kLoop, calls=%fused_computation | loop fusion | flops 262144 | bytes 2097156 | tf_op jit(solution)/shard_map/div | solution.py:416
  96.2 0.6 fusion
Async XLA Ops:
  92.0 0.6 copy-start
where the time goes:
time: 97 us; the launch traced here: 96.8 us
  Pallas kernels  90.1 us (93%)
  other arithmetic  2.86 us (3%)
  local copies, waits for them, and re-layouts  2.49 us (3%)
  between operations  1.34 us (1%)
    pallas_call x1, Pallas kernels, body(): pl.pallas_call(kernel, out_shape=(jax.ShapeDtypeStruct((ROWS, REG), F32),...  90.1 us
    div x1, other arithmetic, body(): scaled = values / jnp.sqrt(totals[4] / total_amps)  2.27 us

commit v1 on v0

v1 whole, which is shorter than its diff:
```python
import functools

import jax
import jax.numpy as jnp
from jax import lax
from jax.experimental import pallas as pl
from jax.experimental.pallas import tpu as pltpu
from jax.sharding import PartitionSpec as P

KEEP_FACTORS = (1.0, 0.9, 1.0, 0.97)
FLIP_FACTORS = (0.9, 1.0, 0.97, 1.0)
QUBITS = 7
REG = 128
MID = 16
PEERS = 64
SECTIONS = 4
BLOCKS = 3
ROWS = 2048
MESH = pl.DeviceIdType.MESH
F32 = jnp.float32
BF16 = jnp.bfloat16


def split(x):
    hi = x.astype(BF16)
    lo = (x - hi.astype(F32)).astype(BF16)
    return hi, lo


def exact_dot(a, b):
    return jnp.dot(a, b, precision=lax.Precision.HIGHEST, preferred_element_type=F32)


def mix_rows(gate_cat, x):
    hi, lo = split(x)
    return jnp.dot(gate_cat, jnp.concatenate([hi, hi, lo], axis=0), preferred_element_type=F32)


def mix_lanes(x, gate_cat):
    hi, lo = split(x)
    return jnp.dot(jnp.concatenate([hi, hi, lo], axis=1), gate_cat, preferred_element_type=F32)


def rows_cat(gate):
    hi, lo = split(gate)
    return jnp.concatenate([hi, lo, hi], axis=1)


def lanes_cat(gate_t):
    hi, lo = split(gate_t)
    return jnp.concatenate([hi, lo, hi], axis=0)


def block_transpose(arrays):
    lane = lax.broadcasted_iota(jnp.int32, arrays[0].shape, 1)
    low_half = lane < 64
    even = (lane // 32) % 2 == 0
    stage = [None] * 4
    for a in range(2):
        moved = pltpu.roll(jnp.where(low_half, arrays[a + 2], arrays[a]), 64, 1)
        stage[a] = jnp.where(low_half, arrays[a], moved)
        stage[a + 2] = jnp.where(low_half, moved, arrays[a + 2])
    result = [None] * 4
    for a in (0, 2):
        result[a] = jnp.where(even, stage[a], pltpu.roll(stage[a + 1], 32, 1))
        result[a + 1] = jnp.where(even, pltpu.roll(stage[a], 96, 1), stage[a + 1])
    return result


def fold_squares(acc, x):
    sq = x * x
    return acc + jnp.sum(sq.reshape(sq.shape[0] // 8, 8, sq.shape[1]), axis=0)


def amp_of(m, j):
    return (m // 8) * 32 + (j // 2) * 16 + (m % 8) * 2 + j % 2


def scalar_pick(kind, table):
    return jnp.where(
        kind == 0,
        F32(table[0]),
        jnp.where(kind == 1, F32(table[1]), jnp.where(kind == 2, F32(table[2]), F32(table[3]))),
    )


def kernel(
    x_ref, gate_ref, kraus_ref, target_ref,
    y_ref, scale_ref, logs_ref,
    all_gates, send1, recv1, mid1, mid2, mid3, recv2, wide2, send3, recv3, h_mats, l_mats, sums_out, sums_in,
    gate_send, gate_recv, pair_send, pair_recv,
    send1_sem, recv1_sem, send2_sem, recv2_sem, send3_sem, recv3_sem, sums_send, sums_recv,
):
    seg = lax.axis_index("segment")
    me = lax.axis_index("amp")
    y_me = me // 16
    z_me = (me % 16) // 2
    core = me % 2
    j_me = (y_me % 2) * 2 + core
    m_me = (y_me // 2) * 8 + z_me
    slot_me = m_me * 4 + j_me
    partner = me + 1 - 2 * core
    zero = jnp.zeros((8, REG), F32)

    def part(index, rows):
        return pl.ds(pl.multiple_of(index * rows, rows), rows)

    def wait_bytes(ref, rows, sem):
        pltpu.make_async_copy(ref.at[pl.ds(0, rows)], ref.at[pl.ds(0, rows)], sem).wait()

    barrier = pltpu.get_barrier_semaphore()

    def greet(k, carry):
        pl.semaphore_signal(barrier, inc=1, device_id=(seg, (me + k) % PEERS), device_id_type=MESH)
        return carry

    lax.fori_loop(1, PEERS, greet, 0)
    for k in range(1, SECTIONS):
        pl.semaphore_signal(barrier, inc=1, device_id=((seg + k) % SECTIONS, me), device_id_type=MESH)

    width = 4

    def pack(k, acc):
        for i in range(width):
            m = k * width + i
            x = x_ref[pl.ds(m, REG, stride=MID), :]
            acc = fold_squares(acc, x)
            pieces = block_transpose([x[q * 32 : (q + 1) * 32] for q in range(4)])
            for j in range(4):
                send1[part(m * 4 + j, 32), :] = pieces[j]
        return acc

    first_sum = lax.fori_loop(0, MID // width, pack, zero)
    all_gates[seg] = gate_ref[0]

    pl.semaphore_wait(barrier, PEERS - 1 + SECTIONS - 1)

    distances = (4, 5, 3, 6, 2, 7, 1, 0)

    def to_all(send_one):
        for dz in distances:
            def one(n, carry, dz=dz):
                z = (z_me + dz) % 8
                y = (y_me + n // 2) % 4
                c = (core + n) % 2
                send_one(y, z, c)
                return carry

            lax.fori_loop(0 if dz else 1, 8, one, 0)

    def send_piece1(y, z, c):
        piece = ((y // 2) * 8 + z) * 4 + (y % 2) * 2 + c
        pltpu.make_async_remote_copy(
            send1.at[part(piece, 32)], recv1.at[part(me, 32)], send1_sem, recv1_sem.at[z_me],
            device_id=(seg, y * 16 + z * 2 + c), device_id_type=MESH,
        ).start()

    to_all(send_piece1)
    recv1[part(me, 32), :] = send1[part(slot_me, 32), :]

    my_half = pl.ds(pl.multiple_of(core * 64, 64), 64)
    other_half = pl.ds(pl.multiple_of((1 - core) * 64, 64), 64)

    def gate_copy(section, target_seg):
        return pltpu.make_async_remote_copy(
            gate_ref.at[0, :, my_half, :],
            all_gates.at[section, :, my_half, :],
            gate_send.at[target_seg],
            gate_recv.at[section],
            device_id=(target_seg, me),
            device_id_type=MESH,
        )

    def pair_copy(section):
        return pltpu.make_async_remote_copy(
            all_gates.at[section, :, my_half, :],
            all_gates.at[section, :, my_half, :],
            pair_send.at[section],
            pair_recv.at[section],
            device_id=(seg, partner),
            device_id_type=MESH,
        )

    def send_gates(section):
        @pl.when(seg == section)
        def _():
            for k in range(1, SECTIONS):
                gate_copy(section, (seg + k) % SECTIONS).start()

    def pass_gates(section):
        @pl.when(seg != section)
        def _():
            gate_copy(section, section).wait_recv()
            pair_copy(section).start()

    def end_gates(section):
        @pl.when(seg != section)
        def _():
            pltpu.make_async_copy(
                all_gates.at[section, :, other_half, :], all_gates.at[section, :, other_half, :], pair_recv.at[section]
            ).wait()

    row = lax.broadcasted_iota(jnp.int32, (REG, REG), 0)
    col = lax.broadcasted_iota(jnp.int32, (REG, REG), 1)
    identity = (row == col).astype(F32)
    to_split = (col == (row % 64) * 2 + row // 64).astype(F32)
    from_split = (row == (col % 64) * 2 + col // 64).astype(F32)

    def noise(section, block):
        product = jnp.ones((REG, REG), F32)
        for q in range(QUBITS):
            kind = kraus_ref[0, section, block, q]
            bit = lax.shift_right_logical(row, QUBITS - 1 - q) & 1
            product = product * jnp.where(bit == 1, scalar_pick(kind, FLIP_FACTORS), scalar_pick(kind, KEEP_FACTORS))
        return product

    def compose(section):
        low, high = identity, identity
        for block in range(BLOCKS):
            on_low = target_ref[section, block] == 0
            gate = all_gates[section, block]
            if block == 0:
                mixed = gate
            else:
                mixed = exact_dot(gate, jnp.where(on_low, low, high))
            mixed = noise(section, block) * mixed
            low, high = jnp.where(on_low, mixed, low), jnp.where(on_low, high, mixed)
        return low, high

    for section in range(SECTIONS):
        send_gates(section)
    for section in range(SECTIONS):
        pass_gates(section)
    low_all = None
    for section in range(SECTIONS):
        end_gates(section)
        low, high = compose(section)
        if section > 0:
            high = exact_dot(high, from_split)
        if section == 3:
            high = exact_dot(to_split, high)
        h_mats[section] = rows_cat(high)
        low_all = low if section == 0 else exact_dot(low, low_all)
        l_mats[section] = lanes_cat(low_all.T)

    def split_rows(ref, index, stride, rows=64):
        return jnp.concatenate(
            [ref[pl.ds(2 * index, rows, stride=stride), :], ref[pl.ds(2 * index + 1, rows, stride=stride), :]], axis=0
        )

    def arrived(ref, sem, z):
        @pl.when(z == z_me)
        def _():
            wait_bytes(ref, 7 * 32, sem.at[z])

        @pl.when(z != z_me)
        def _():
            wait_bytes(ref, 8 * 32, sem.at[z])

    def source_z(k):
        dz = jnp.where(k % 2 == 1, 4 + (k + 1) // 2, 4 - k // 2)
        return (z_me + 8 - dz) % 8

    def section0(k, carry):
        z = source_z(k)
        arrived(recv1, recv1_sem, z)
        kappas = [z * 2, z * 2 + 1]
        tall = []
        for kappa in kappas:
            parts = block_transpose([recv1[part(y * 16 + kappa, 32), :] for y in range(4)])
            tall.append(jnp.concatenate(parts, axis=0))
        wide = mix_rows(h_mats[0], jnp.concatenate(tall, axis=1))
        for i, kappa in enumerate(kappas):
            parts = block_transpose([wide[q * 32 : (q + 1) * 32, i * REG : (i + 1) * REG] for q in range(4)])
            for y in range(4):
                mid1[part(y * 16 + kappa, 32), :] = parts[y]
        return carry

    lax.fori_loop(0, 8, section0, 0)
    step = 4

    def section1(k, carry):
        rs = [k * step + i for i in range(step)]
        wide = mix_rows(h_mats[1], jnp.concatenate([split_rows(mid1, r, 32) for r in rs], axis=1))
        for i, r in enumerate(rs):
            parts = block_transpose([wide[y * 32 : (y + 1) * 32, i * REG : (i + 1) * REG] for y in range(4)])
            for q in range(4):
                mid2[part(q * 16 + r, 32), :] = parts[q]
        return carry

    lax.fori_loop(0, 16 // step, section1, 0)

    def section2(k, carry):
        kappas = [k * step + i for i in range(step)]
        wide = mix_rows(h_mats[2], jnp.concatenate([split_rows(mid2, kappa, 32) for kappa in kappas], axis=1))
        for i, kappa in enumerate(kappas):
            parts = block_transpose([wide[q * 32 : (q + 1) * 32, i * REG : (i + 1) * REG] for q in range(4)])
            for y in range(4):
                mid3[part(y * 16 + kappa, 32), :] = parts[y]
        return carry

    lax.fori_loop(0, 16 // step, section2, 0)

    mid2_tiles = mid2.reshape(64, 32, REG)
    recv2_tiles = recv2.reshape(4, 64, 8, REG)

    def send_quarter(k, carry):
        j = (j_me + k) % 4
        pltpu.make_async_remote_copy(
            mid2_tiles.at[:, part(j, 8), :], recv2_tiles.at[j_me], send2_sem, recv2_sem,
            device_id=(seg, (m_me // 8) * 32 + (j // 2) * 16 + z_me * 2 + j % 2), device_id_type=MESH,
        ).start()
        return carry

    lax.fori_loop(1, 4, send_quarter, 0)

    def section3(k, carry):
        rs = [k * step + i for i in range(step)]
        wide = mix_rows(h_mats[3], jnp.concatenate([split_rows(mid3, r, 32) for r in rs], axis=1))
        for i, r in enumerate(rs):
            here = wide[:, i * REG : (i + 1) * REG]
            send3[pl.ds(2 * r, 64, stride=32), :] = here[:64]
            send3[pl.ds(2 * r + 1, 64, stride=32), :] = here[64:]
        return carry

    lax.fori_loop(0, 16 // step, section3, 0)

    def send_piece3(y, z, c):
        to = y * 16 + z * 2 + c
        pltpu.make_async_remote_copy(
            send3.at[part(to, 32)], recv3.at[part(slot_me, 32)], send3_sem, recv3_sem.at[z_me],
            device_id=(seg, to), device_id_type=MESH,
        ).start()

    to_all(send_piece3)
    recv3[part(slot_me, 32), :] = send3[part(me, 32), :]

    def norm0(k, acc):
        xs = [x_ref[pl.ds(k * step + i, REG, stride=MID), :] for i in range(step)]
        wide = mix_rows(h_mats[0], jnp.concatenate(xs, axis=1))
        tall = jnp.concatenate([wide[:, i * REG : (i + 1) * REG] for i in range(step)], axis=0)
        return fold_squares(acc, mix_lanes(tall, l_mats[0]))

    sum0 = lax.fori_loop(0, MID // step, norm0, zero)
    wait_bytes(recv2, 3 * 512, recv2_sem)
    for n in range(4):
        recv2_tiles[j_me, n * 16 : (n + 1) * 16] = mid2_tiles[n * 16 : (n + 1) * 16, part(j_me, 8), :]

    def norm1(k, acc):
        parts = block_transpose([recv2[part(j * 4 + k, REG), :] for j in range(4)])
        for y in range(4):
            wide2[part(y * 4 + k, REG), :] = parts[y]
        return fold_squares(acc, mix_lanes(jnp.concatenate(parts, axis=0), l_mats[1]))

    sum1 = lax.fori_loop(0, 4, norm1, zero)

    def norm2(k, acc):
        xs = [split_rows(wide2.at[part(k, 512)], i, 8) for i in range(4)]
        wide = mix_rows(h_mats[2], jnp.concatenate(xs, axis=1))
        tall = jnp.concatenate([wide[:, i * REG : (i + 1) * REG] for i in range(4)], axis=0)
        return fold_squares(acc, mix_lanes(tall, l_mats[2]))

    sum2 = lax.fori_loop(0, 4, norm2, zero)

    def last(k, acc):
        z = source_z(k)
        arrived(recv3, recv3_sem, z)
        ms = [z, z + 8]
        tall = []
        for m in ms:
            tall += block_transpose([recv3[part(m * 4 + j, 32), :] for j in range(4)])
        mixed = mix_lanes(jnp.concatenate(tall, axis=0), l_mats[3])
        for i, m in enumerate(ms):
            y_ref[pl.ds(m, REG, stride=MID), :] = mixed[i * REG : (i + 1) * REG]
        return fold_squares(acc, mixed)

    sum3 = lax.fori_loop(0, 8, last, zero)

    lane = lax.broadcasted_iota(jnp.int32, (1, REG), 1)
    line = jnp.ones((1, REG), F32)
    for n, acc in enumerate((first_sum, sum0, sum1, sum2, sum3)):
        line = jnp.where(lane == n, jnp.sum(acc), line)
    sums_out[...] = line
    sums_in[me] = line

    def send_sums(y, z, c):
        pltpu.make_async_remote_copy(
            sums_out, sums_in.at[me], sums_send, sums_recv, device_id=(seg, y * 16 + z * 2 + c), device_id_type=MESH
        ).start()

    to_all(send_sums)

    for section in range(SECTIONS):
        @pl.when(seg == section)
        def _():
            for k in range(1, SECTIONS):
                gate_copy(section, (seg + k) % SECTIONS).wait_send()

        @pl.when(seg != section)
        def _():
            pair_copy(section).wait_send()

    wait_bytes(send1, 63 * 32, send1_sem)
    wait_bytes(recv2, 3 * 512, send2_sem)
    wait_bytes(send3, 63 * 32, send3_sem)
    wait_bytes(sums_in, 63, sums_send)
    wait_bytes(sums_in, 63, sums_recv)
    totals = jnp.sum(sums_in[...], axis=0)
    logs_ref[...] = jnp.log(pltpu.roll(totals, REG - 1, 1) / totals)
    mean = jnp.sum(jnp.where(lane == 4, totals, 0.0)) / (PEERS * ROWS * REG)
    scale_ref[...] = 1.0 / jnp.sqrt(jnp.full((1, REG), mean, F32))


def body(states, gate_blocks, kraus_picks, block_targets):
    dma = pltpu.SemaphoreType.DMA
    vmem = pl.BlockSpec(memory_space=pltpu.VMEM)
    smem = pl.BlockSpec(memory_space=pltpu.SMEM)
    big = pltpu.VMEM((ROWS, REG), F32)
    line = jax.ShapeDtypeStruct((1, REG), F32)
    values, scale, logs = pl.pallas_call(
        kernel,
        out_shape=(jax.ShapeDtypeStruct((ROWS, REG), F32), line, line),
        in_specs=[vmem, vmem, smem, smem],
        out_specs=(vmem, vmem, vmem),
        scratch_shapes=[
            pltpu.VMEM((SECTIONS, BLOCKS, REG, REG), F32),
            big, big, big, big, big, big, big, big, big,
            pltpu.VMEM((SECTIONS, REG, 3 * REG), BF16),
            pltpu.VMEM((SECTIONS, 3 * REG, REG), BF16),
            pltpu.VMEM((1, REG), F32),
            pltpu.VMEM((PEERS, 1, REG), F32),
            dma((SECTIONS,)), dma((SECTIONS,)), dma((SECTIONS,)), dma((SECTIONS,)),
            dma, dma((8,)), dma, dma, dma, dma((8,)), dma, dma,
        ],
        compiler_params=pltpu.CompilerParams(collective_id=0, has_side_effects=True),
        name="trajectory",
    )(states.reshape(ROWS, REG), gate_blocks, kraus_picks, block_targets)
    return (values * scale).reshape(states.shape), logs[:, :SECTIONS]


def solution(mesh):
    in_specs = (
        P("segment", "amp"),
        P("segment", None, None, None),
        P("segment", None, None, None),
        P(),
    )
    out_specs = (P("segment", "amp"), P("segment", None))
    return jax.shard_map(body, mesh=mesh, in_specs=in_specs, out_specs=out_specs, check_vma=False)
```

time: 97 us -> 87 us (0.90)
  Pallas kernels: 90.1 us -> 80.8 us
    pallas_call x1, Pallas kernels: 90.1 us -> 80.8 us  [body(): pl.pallas_call(kernel, out_shape=(jax.ShapeDtypeStruct((ROWS, REG), F32),...]
    unnamed x2 -> x6, local copies, waits for them, and re-layouts: 0.62 us -> 3.04 us
    div x1 -> x0, other arithmetic: 2.27 us -> none  [body(): scaled = values / jnp.sqrt(totals[4] / total_amps)]
    mul x0 -> x1, other arithmetic: none -> 2.26 us  [body(): return ((values * scale).reshape(states.shape), logs[:, :SECTIONS])]
    squeeze x1 -> x0, local copies, waits for them, and re-layouts: 1.29 us -> none  [body(): kraus_picks[0]]
where the time goes in v1:
time: 87 us; the launch traced here: 86.8 us
  Pallas kernels  80.8 us (93%)
  local copies, waits for them, and re-layouts  3.04 us (3%)
  other arithmetic  2.26 us (3%)
    pallas_call x1, Pallas kernels, body(): pl.pallas_call(kernel, out_shape=(jax.ShapeDtypeStruct((ROWS, REG), F32),...  80.8 us
    unnamed x6, local copies, waits for them, and re-layouts  3.04 us
    mul x1, other arithmetic, body(): return ((values * scale).reshape(states.shape), logs[:, :SECTIONS])  2.26 us

profile of v1, /device:TPU:1, one launch (start us, length us, event | category | flops | bytes accessed | tf_op | source)
XLA Modules:
  0.0 86.8 jit_solution(301509520848708554)
XLA Ops:
  0.6 1.3 %copy.6.kraus_ref = s32[1,4,3,7]{3,2,1,0:T(4,128)} copy(s32[1,4,3,7]{3,1,2,0:T(4,128)} %param.6) | data formatting | bytes 672 | tf_op args[2]
  1.9 80.8 %trajectory.1 = (f32[2048,128]{1,0:T(8,128)}, f32[1,128]{1,0:T(1,128)}, f32[1,128]{1,0:T(1,128)}) custom-call(f32[2048,128]{1,0:T(8,128)} %bitcast.5, f32[1,3,128,128]{3,2,1,0:T(8,128)} %gate_ref.1, s32[1,4,3,7]{3,2,1,0:T(4,128)} %copy.6.kraus_ref, s32[4,3]{1,0:T(4,128)} %target_ref.1), custom_call_target="tpu_custom_call" | custom-call | tf_op jit(solution)/shard_map/trajectory/pallas_call | solution.py:420
  82.8 0.0 copy-start
  82.8 0.7 copy-done
  83.4 2.3 %broadcast_multiply_fusion = f32[2048,128]{1,0:T(8,128)} fusion(f32[2048,128]{1,0:T(8,128)} %get-tuple-element.5, f32[128]{0:T(128)S(1)} %bitcast.6), kind=kLoop, calls=%fused_computation | loop fusion | flops 262144 | bytes 2097664 | tf_op jit(solution)/shard_map/mul | solution.py:438
  85.7 0.0 copy-start.1
  85.7 0.6 copy-done.1
  86.3 0.5 copy.8
Async XLA Ops:
  82.8 0.7 copy-start
  85.7 0.6 copy-start.1

commit v2 on v1

--- a/solution.py
+++ b/solution.py
@@ -85,11 +85,12 @@
 
 
 def kernel(
-    x_ref, gate_ref, kraus_ref, target_ref,
+    states_ref, gate_ref, kraus_ref, target_ref,
     y_ref, scale_ref, logs_ref,
-    all_gates, send1, recv1, mid1, mid2, mid3, recv2, wide2, send3, recv3, h_mats, l_mats, sums_out, sums_in,
+    x_ref, all_gates, send1, recv1, mid1, mid2, mid3, recv2, wide2, send3, recv3, h_mats, l_mats, sums_out, sums_in,
     gate_send, gate_recv, pair_send, pair_recv,
     send1_sem, recv1_sem, send2_sem, recv2_sem, send3_sem, recv3_sem, sums_send, sums_recv,
+    load_sems,
 ):
     seg = lax.axis_index("segment")
     me = lax.axis_index("amp")
@@ -108,13 +109,27 @@
     def wait_bytes(ref, rows, sem):
         pltpu.make_async_copy(ref.at[pl.ds(0, rows)], ref.at[pl.ds(0, rows)], sem).wait()
 
+    load_states = pltpu.make_async_copy(states_ref, x_ref, load_sems.at[0])
+    load_gates = pltpu.make_async_copy(gate_ref.at[0], all_gates.at[seg], load_sems.at[1])
+    load_states.start()
+    load_gates.start()
+
+    distances = (4, 5, 3, 6, 2, 7, 1, 0)
+
+    def to_all(send_one, wanted=distances):
+        for dz in wanted:
+            def one(n, carry, dz=dz):
+                send_one((y_me + n // 2) % 4, (z_me + dz) % 8, (core + n) % 2)
+                return carry
+
+            lax.fori_loop(0 if dz else 1, 8, one, 0)
+
     barrier = pltpu.get_barrier_semaphore()
 
-    def greet(k, carry):
-        pl.semaphore_signal(barrier, inc=1, device_id=(seg, (me + k) % PEERS), device_id_type=MESH)
-        return carry
-
-    lax.fori_loop(1, PEERS, greet, 0)
+    def greet(y, z, c):
+        pl.semaphore_signal(barrier, inc=1, device_id=(seg, y * 16 + z * 2 + c), device_id_type=MESH)
+
+    to_all(greet)
     for k in range(1, SECTIONS):
         pl.semaphore_signal(barrier, inc=1, device_id=((seg + k) % SECTIONS, me), device_id_type=MESH)
 
@@ -130,32 +145,28 @@
                 send1[part(m * 4 + j, 32), :] = pieces[j]
         return acc
 
+    load_states.wait()
     first_sum = lax.fori_loop(0, MID // width, pack, zero)
-    all_gates[seg] = gate_ref[0]
+    load_gates.wait()
 
     pl.semaphore_wait(barrier, PEERS - 1 + SECTIONS - 1)
 
-    distances = (4, 5, 3, 6, 2, 7, 1, 0)
-
-    def to_all(send_one):
-        for dz in distances:
-            def one(n, carry, dz=dz):
-                z = (z_me + dz) % 8
-                y = (y_me + n // 2) % 4
-                c = (core + n) % 2
-                send_one(y, z, c)
-                return carry
-
-            lax.fori_loop(0 if dz else 1, 8, one, 0)
-
-    def send_piece1(y, z, c):
-        piece = ((y // 2) * 8 + z) * 4 + (y % 2) * 2 + c
-        pltpu.make_async_remote_copy(
-            send1.at[part(piece, 32)], recv1.at[part(me, 32)], send1_sem, recv1_sem.at[z_me],
-            device_id=(seg, y * 16 + z * 2 + c), device_id_type=MESH,
-        ).start()
-
-    to_all(send_piece1)
+    def exchange(source, target, piece_of, slot, send_sem, recv_sem):
+        def one(y, z, c):
+            pltpu.make_async_remote_copy(
+                source.at[part(piece_of(y, z, c), 32)], target.at[part(slot, 32)], send_sem, recv_sem.at[z_me],
+                device_id=(seg, y * 16 + z * 2 + c), device_id_type=MESH,
+            ).start()
+
+        to_all(one)
+
+    def piece_by_m(y, z, c):
+        return ((y // 2) * 8 + z) * 4 + (y % 2) * 2 + c
+
+    def piece_by_g(y, z, c):
+        return y * 16 + z * 2 + c
+
+    exchange(send1, recv1, piece_by_m, me, send1_sem, recv1_sem)
     recv1[part(me, 32), :] = send1[part(slot_me, 32), :]
 
     my_half = pl.ds(pl.multiple_of(core * 64, 64), 64)
@@ -163,7 +174,7 @@
 
     def gate_copy(section, target_seg):
         return pltpu.make_async_remote_copy(
-            gate_ref.at[0, :, my_half, :],
+            all_gates.at[section, :, my_half, :],
             all_gates.at[section, :, my_half, :],
             gate_send.at[target_seg],
             gate_recv.at[section],
@@ -209,7 +220,7 @@
     def noise(section, block):
         product = jnp.ones((REG, REG), F32)
         for q in range(QUBITS):
-            kind = kraus_ref[0, section, block, q]
+            kind = kraus_ref[0, block, section, q]
             bit = lax.shift_right_logical(row, QUBITS - 1 - q) & 1
             product = product * jnp.where(bit == 1, scalar_pick(kind, FLIP_FACTORS), scalar_pick(kind, KEEP_FACTORS))
         return product
@@ -325,14 +336,7 @@
 
     lax.fori_loop(0, 16 // step, section3, 0)
 
-    def send_piece3(y, z, c):
-        to = y * 16 + z * 2 + c
-        pltpu.make_async_remote_copy(
-            send3.at[part(to, 32)], recv3.at[part(slot_me, 32)], send3_sem, recv3_sem.at[z_me],
-            device_id=(seg, to), device_id_type=MESH,
-        ).start()
-
-    to_all(send_piece3)
+    exchange(send3, recv3, piece_by_g, slot_me, send3_sem, recv3_sem)
     recv3[part(slot_me, 32), :] = send3[part(me, 32), :]
 
     def norm0(k, acc):
@@ -411,18 +415,32 @@
     scale_ref[...] = 1.0 / jnp.sqrt(jnp.full((1, REG), mean, F32))
 
 
+def scale_kernel(values_ref, scale_ref, logs_ref, y_ref, log_weights_ref, scaled, sems):
+    log_weights_ref[...] = logs_ref[:, :SECTIONS]
+    rows = ROWS // 4
+    for n in range(4):
+        part = pl.ds(n * rows, rows)
+        scaled[part, :] = values_ref[part, :] * scale_ref[...]
+        pltpu.make_async_copy(scaled.at[part], y_ref.at[part], sems.at[n]).start()
+    for n in range(4):
+        part = pl.ds(n * rows, rows)
+        pltpu.make_async_copy(scaled.at[part], y_ref.at[part], sems.at[n]).wait()
+
+
 def body(states, gate_blocks, kraus_picks, block_targets):
     dma = pltpu.SemaphoreType.DMA
     vmem = pl.BlockSpec(memory_space=pltpu.VMEM)
     smem = pl.BlockSpec(memory_space=pltpu.SMEM)
+    anywhere = pl.BlockSpec(memory_space=pl.ANY)
     big = pltpu.VMEM((ROWS, REG), F32)
-    line = jax.ShapeDtypeStruct((1, REG), F32)
+    line = pltpu.VMEM((1, REG), F32)
     values, scale, logs = pl.pallas_call(
         kernel,
-        out_shape=(jax.ShapeDtypeStruct((ROWS, REG), F32), line, line),
-        in_specs=[vmem, vmem, smem, smem],
+        out_shape=(big, line, line),
+        in_specs=[anywhere, anywhere, smem, smem],
         out_specs=(vmem, vmem, vmem),
         scratch_shapes=[
+            big,
             pltpu.VMEM((SECTIONS, BLOCKS, REG, REG), F32),
             big, big, big, big, big, big, big, big, big,
             pltpu.VMEM((SECTIONS, REG, 3 * REG), BF16),
@@ -431,11 +449,21 @@
             pltpu.VMEM((PEERS, 1, REG), F32),
             dma((SECTIONS,)), dma((SECTIONS,)), dma((SECTIONS,)), dma((SECTIONS,)),
             dma, dma((8,)), dma, dma, dma, dma((8,)), dma, dma,
+            dma((2,)),
         ],
         compiler_params=pltpu.CompilerParams(collective_id=0, has_side_effects=True),
         name="trajectory",
-    )(states.reshape(ROWS, REG), gate_blocks, kraus_picks, block_targets)
-    return (values * scale).reshape(states.shape), logs[:, :SECTIONS]
+    )(states.reshape(ROWS, REG), gate_blocks, kraus_picks.transpose(0, 2, 1, 3), block_targets)
+    final, log_weights = pl.pallas_call(
+        scale_kernel,
+        out_shape=(jax.ShapeDtypeStruct((ROWS, REG), F32), jax.ShapeDtypeStruct((1, SECTIONS), F32)),
+        in_specs=[vmem, vmem, vmem],
+        out_specs=(anywhere, vmem),
+        scratch_shapes=[big, dma((4,))],
+        compiler_params=pltpu.CompilerParams(vmem_limit_bytes=8 * 2**20),
+        name="scale",
+    )(values, scale, logs)
+    return final.reshape(states.shape), log_weights
 
 
 def solution(mesh):

time: 87 us -> 82 us (0.943)
  local copies, waits for them, and re-layouts: 3.04 us -> 0 us
  other arithmetic: 2.26 us -> 0 us
    unnamed x6 -> x0, local copies, waits for them, and re-layouts: 3.04 us -> none
    mul x1 -> x0, other arithmetic: 2.26 us -> none  [body(): return ((values * scale).reshape(states.shape), logs[:, :SECTIONS])]
    pallas_call x1 -> x2, Pallas kernels: 80.8 us -> 81.2 us  [the longest x1 79.7 us: body(): pl.pallas_call(kernel, out_shape=(big, line, line), in_specs=[anywhere, a...]
where the time goes in v2:
time: 82 us; the launch traced here: 81.9 us
  Pallas kernels  81.2 us (99%)
    pallas_call x1, Pallas kernels, body(): pl.pallas_call(kernel, out_shape=(big, line, line), in_specs=[anywhere, a...  79.7 us

profile of v2, /device:TPU:1, one launch (start us, length us, event | category | flops | bytes accessed | tf_op | source)
XLA Modules:
  0.0 81.9 jit_solution(4772510698444151139)
XLA Ops:
  0.6 79.7 %trajectory.1 = (f32[2048,128]{1,0:T(8,128)S(1)}, f32[1,128]{1,0:T(1,128)S(1)}, f32[1,128]{1,0:T(1,128)S(1)}) custom-call(f32[2048,128]{1,0:T(8,128)} %bitcast.3, f32[1,3,128,128]{3,2,1,0:T(8,128)} %gate_ref.1, s32[1,3,4,7]{3,2,1,0:T(4,128)} %bitcast.4, s32[4,3]{1,0:T(4,128)} %target_ref.1), custom_call_target="tpu_custom_call" | custom-call | tf_op jit(solution)/shard_map/trajectory/pallas_call | solution.py:437
  80.3 1.5 %scale.1 = (f32[2048,128]{1,0:T(8,128)}, f32[1,4]{1,0:T(1,128)}) custom-call(f32[2048,128]{1,0:T(8,128)S(1)} %get-tuple-element.7.values_ref, f32[1,128]{1,0:T(1,128)S(1)} %get-tuple-element.8.scale_ref, f32[1,128]{1,0:T(1,128)S(1)} %get-tuple-element.9.logs_ref), custom_call_target="tpu_custom_call" | custom-call | tf_op jit(solution)/shard_map/scale/pallas_call | solution.py:457

commit v3 on v2

--- a/solution.py
+++ b/solution.py
@@ -85,9 +85,9 @@
 
 
 def kernel(
-    states_ref, gate_ref, kraus_ref, target_ref,
+    states_ref, gate_ref, kraus_hbm, target_hbm,
     y_ref, scale_ref, logs_ref,
-    x_ref, all_gates, send1, recv1, mid1, mid2, mid3, recv2, wide2, send3, recv3, h_mats, l_mats, sums_out, sums_in,
+    kraus_ref, target_ref, x_ref, all_gates, send1, recv1, mid1, mid2, mid3, recv2, wide2, send3, recv3, h_mats, l_mats, sums_out, sums_in,
     gate_send, gate_recv, pair_send, pair_recv,
     send1_sem, recv1_sem, send2_sem, recv2_sem, send3_sem, recv3_sem, sums_send, sums_recv,
     load_sems,
@@ -100,6 +100,7 @@
     j_me = (y_me % 2) * 2 + core
     m_me = (y_me // 2) * 8 + z_me
     slot_me = m_me * 4 + j_me
+    kappa_me = me // 4
     partner = me + 1 - 2 * core
     zero = jnp.zeros((8, REG), F32)
 
@@ -109,31 +110,42 @@
     def wait_bytes(ref, rows, sem):
         pltpu.make_async_copy(ref.at[pl.ds(0, rows)], ref.at[pl.ds(0, rows)], sem).wait()
 
-    load_states = pltpu.make_async_copy(states_ref, x_ref, load_sems.at[0])
-    load_gates = pltpu.make_async_copy(gate_ref.at[0], all_gates.at[seg], load_sems.at[1])
-    load_states.start()
-    load_gates.start()
-
-    distances = (4, 5, 3, 6, 2, 7, 1, 0)
-
-    def to_all(send_one, wanted=distances):
-        for dz in wanted:
-            def one(n, carry, dz=dz):
-                send_one((y_me + n // 2) % 4, (z_me + dz) % 8, (core + n) % 2)
-                return carry
-
-            lax.fori_loop(0 if dz else 1, 8, one, 0)
+    loads = [
+        pltpu.make_async_copy(states_ref, x_ref, load_sems.at[0]),
+        pltpu.make_async_copy(gate_ref.at[0], all_gates.at[seg], load_sems.at[1]),
+        pltpu.make_async_copy(kraus_hbm, kraus_ref, load_sems.at[2]),
+        pltpu.make_async_copy(target_hbm, target_ref, load_sems.at[3]),
+    ]
+    for load in loads:
+        load.start()
 
     barrier = pltpu.get_barrier_semaphore()
 
-    def greet(y, z, c):
-        pl.semaphore_signal(barrier, inc=1, device_id=(seg, y * 16 + z * 2 + c), device_id_type=MESH)
-
-    to_all(greet)
+    def greet(k, carry):
+        pl.semaphore_signal(barrier, inc=1, device_id=(seg, (me + k) % PEERS), device_id_type=MESH)
+        return carry
+
+    lax.fori_loop(40, PEERS, greet, 0)
+    lax.fori_loop(1, 40, greet, 0)
     for k in range(1, SECTIONS):
         pl.semaphore_signal(barrier, inc=1, device_id=((seg + k) % SECTIONS, me), device_id_type=MESH)
 
-    width = 4
+    far_first = ((1, 0), (1, 1), (0, 1), (0, 0))
+    near_first = far_first[::-1]
+
+    def to_all(send_one, flips=far_first):
+        for flip_upper, flip_lower in flips:
+            y = ((y_me // 2 + flip_upper) % 2) * 2 + (y_me + flip_lower) % 2
+            for on in (2, 1, 3, 0):
+                pair = (z_me // 2 + on) % 4
+
+                def one(n, carry, y=y, pair=pair):
+                    send_one(y, pair * 2 + (z_me + n // 2) % 2, (core + n) % 2)
+                    return carry
+
+                lax.fori_loop(0 if flip_upper or flip_lower or on else 1, 4, one, 0)
+
+    width = 16
 
     def pack(k, acc):
         for i in range(width):
@@ -145,20 +157,21 @@
                 send1[part(m * 4 + j, 32), :] = pieces[j]
         return acc
 
-    load_states.wait()
+    loads[0].wait()
     first_sum = lax.fori_loop(0, MID // width, pack, zero)
-    load_gates.wait()
+    for load in loads[1:]:
+        load.wait()
 
     pl.semaphore_wait(barrier, PEERS - 1 + SECTIONS - 1)
 
-    def exchange(source, target, piece_of, slot, send_sem, recv_sem):
+    def exchange(source, target, piece_of, slot, send_sem, recv_sem, group, flips):
         def one(y, z, c):
             pltpu.make_async_remote_copy(
-                source.at[part(piece_of(y, z, c), 32)], target.at[part(slot, 32)], send_sem, recv_sem.at[z_me],
+                source.at[part(piece_of(y, z, c), 32)], target.at[part(slot, 32)], send_sem, recv_sem.at[group],
                 device_id=(seg, y * 16 + z * 2 + c), device_id_type=MESH,
             ).start()
 
-        to_all(one)
+        to_all(one, flips)
 
     def piece_by_m(y, z, c):
         return ((y // 2) * 8 + z) * 4 + (y % 2) * 2 + c
@@ -166,7 +179,7 @@
     def piece_by_g(y, z, c):
         return y * 16 + z * 2 + c
 
-    exchange(send1, recv1, piece_by_m, me, send1_sem, recv1_sem)
+    exchange(send1, recv1, piece_by_m, me, send1_sem, recv1_sem, kappa_me, far_first)
     recv1[part(me, 32), :] = send1[part(slot_me, 32), :]
 
     my_half = pl.ds(pl.multiple_of(core * 64, 64), 64)
@@ -216,6 +229,7 @@
     identity = (row == col).astype(F32)
     to_split = (col == (row % 64) * 2 + row // 64).astype(F32)
     from_split = (row == (col % 64) * 2 + col // 64).astype(F32)
+    to_lanes = (col == (row % 32 // 2) * 8 + (row // 32) * 2 + row % 2).astype(F32)
 
     def noise(section, block):
         product = jnp.ones((REG, REG), F32)
@@ -248,8 +262,8 @@
         low, high = compose(section)
         if section > 0:
             high = exact_dot(high, from_split)
-        if section == 3:
-            high = exact_dot(to_split, high)
+        if section % 2 == 1:
+            high = exact_dot(to_lanes if section == 1 else to_split, high)
         h_mats[section] = rows_cat(high)
         low_all = low if section == 0 else exact_dot(low, low_all)
         l_mats[section] = lanes_cat(low_all.T)
@@ -259,42 +273,39 @@
             [ref[pl.ds(2 * index, rows, stride=stride), :], ref[pl.ds(2 * index + 1, rows, stride=stride), :]], axis=0
         )
 
-    def arrived(ref, sem, z):
-        @pl.when(z == z_me)
-        def _():
-            wait_bytes(ref, 7 * 32, sem.at[z])
-
-        @pl.when(z != z_me)
-        def _():
-            wait_bytes(ref, 8 * 32, sem.at[z])
-
-    def source_z(k):
-        dz = jnp.where(k % 2 == 1, 4 + (k + 1) // 2, 4 - k // 2)
-        return (z_me + 8 - dz) % 8
+    def arrived(ref, sem, group, own):
+        @pl.when(group == own)
+        def _():
+            wait_bytes(ref, 3 * 32, sem.at[group])
+
+        @pl.when(group != own)
+        def _():
+            wait_bytes(ref, 4 * 32, sem.at[group])
 
     def section0(k, carry):
-        z = source_z(k)
-        arrived(recv1, recv1_sem, z)
-        kappas = [z * 2, z * 2 + 1]
+        flip, half = k // 2, k % 2
+        y = ((y_me // 2 + 1 - flip // 2) % 2) * 2 + (y_me + (flip + 1) // 2) % 2
+        kappas = [y * 4 + (z_me // 2 + 4 - on) % 4 for on in (2 + half, 1 - half)]
         tall = []
         for kappa in kappas:
-            parts = block_transpose([recv1[part(y * 16 + kappa, 32), :] for y in range(4)])
+            arrived(recv1, recv1_sem, kappa, kappa_me)
+            parts = block_transpose([recv1[part(kappa * 4 + n, 32), :] for n in range(4)])
             tall.append(jnp.concatenate(parts, axis=0))
         wide = mix_rows(h_mats[0], jnp.concatenate(tall, axis=1))
         for i, kappa in enumerate(kappas):
             parts = block_transpose([wide[q * 32 : (q + 1) * 32, i * REG : (i + 1) * REG] for q in range(4)])
-            for y in range(4):
-                mid1[part(y * 16 + kappa, 32), :] = parts[y]
+            for n in range(4):
+                mid1[part(kappa * 4 + n, 32), :] = parts[n]
         return carry
 
     lax.fori_loop(0, 8, section0, 0)
-    step = 4
+    step = 16
 
     def section1(k, carry):
         rs = [k * step + i for i in range(step)]
         wide = mix_rows(h_mats[1], jnp.concatenate([split_rows(mid1, r, 32) for r in rs], axis=1))
         for i, r in enumerate(rs):
-            parts = block_transpose([wide[y * 32 : (y + 1) * 32, i * REG : (i + 1) * REG] for y in range(4)])
+            parts = block_transpose([wide[n * 32 : (n + 1) * 32, i * REG : (i + 1) * REG] for n in range(4)])
             for q in range(4):
                 mid2[part(q * 16 + r, 32), :] = parts[q]
         return carry
@@ -306,8 +317,8 @@
         wide = mix_rows(h_mats[2], jnp.concatenate([split_rows(mid2, kappa, 32) for kappa in kappas], axis=1))
         for i, kappa in enumerate(kappas):
             parts = block_transpose([wide[q * 32 : (q + 1) * 32, i * REG : (i + 1) * REG] for q in range(4)])
-            for y in range(4):
-                mid3[part(y * 16 + kappa, 32), :] = parts[y]
+            for n in range(4):
+                mid3[part(kappa * 4 + n, 32), :] = parts[n]
         return carry
 
     lax.fori_loop(0, 16 // step, section2, 0)
@@ -336,8 +347,10 @@
 
     lax.fori_loop(0, 16 // step, section3, 0)
 
-    exchange(send3, recv3, piece_by_g, slot_me, send3_sem, recv3_sem)
+    exchange(send3, recv3, piece_by_g, slot_me, send3_sem, recv3_sem, m_me, near_first)
     recv3[part(slot_me, 32), :] = send3[part(me, 32), :]
+
+    step = 4
 
     def norm0(k, acc):
         xs = [x_ref[pl.ds(k * step + i, REG, stride=MID), :] for i in range(step)]
@@ -367,11 +380,13 @@
     sum2 = lax.fori_loop(0, 4, norm2, zero)
 
     def last(k, acc):
-        z = source_z(k)
-        arrived(recv3, recv3_sem, z)
-        ms = [z, z + 8]
+        on = k % 4
+        pair = (z_me // 2 + jnp.where(on < 2, on + 2, 3 - on)) % 4
+        upper = (y_me // 2 + k // 4) % 2
+        ms = [upper * 8 + pair * 2, upper * 8 + pair * 2 + 1]
         tall = []
         for m in ms:
+            arrived(recv3, recv3_sem, m, m_me)
             tall += block_transpose([recv3[part(m * 4 + j, 32), :] for j in range(4)])
         mixed = mix_lanes(jnp.concatenate(tall, axis=0), l_mats[3])
         for i, m in enumerate(ms):
@@ -430,16 +445,17 @@
 def body(states, gate_blocks, kraus_picks, block_targets):
     dma = pltpu.SemaphoreType.DMA
     vmem = pl.BlockSpec(memory_space=pltpu.VMEM)
-    smem = pl.BlockSpec(memory_space=pltpu.SMEM)
     anywhere = pl.BlockSpec(memory_space=pl.ANY)
     big = pltpu.VMEM((ROWS, REG), F32)
     line = pltpu.VMEM((1, REG), F32)
     values, scale, logs = pl.pallas_call(
         kernel,
         out_shape=(big, line, line),
-        in_specs=[anywhere, anywhere, smem, smem],
+        in_specs=[anywhere] * 4,
         out_specs=(vmem, vmem, vmem),
         scratch_shapes=[
+            pltpu.SMEM((1, BLOCKS, SECTIONS, QUBITS), jnp.int32),
+            pltpu.SMEM((SECTIONS, BLOCKS), jnp.int32),
             big,
             pltpu.VMEM((SECTIONS, BLOCKS, REG, REG), F32),
             big, big, big, big, big, big, big, big, big,
@@ -448,8 +464,8 @@
             pltpu.VMEM((1, REG), F32),
             pltpu.VMEM((PEERS, 1, REG), F32),
             dma((SECTIONS,)), dma((SECTIONS,)), dma((SECTIONS,)), dma((SECTIONS,)),
-            dma, dma((8,)), dma, dma, dma, dma((8,)), dma, dma,
-            dma((2,)),
+            dma, dma((16,)), dma, dma, dma, dma((16,)), dma, dma,
+            dma((4,)),
         ],
         compiler_params=pltpu.CompilerParams(collective_id=0, has_side_effects=True),
         name="trajectory",

time: 82 us -> 78.2 us (0.954)
  Pallas kernels: 81.2 us -> 77.5 us
    pallas_call x1, Pallas kernels: 79.7 us -> 76 us  [body(): pl.pallas_call(kernel, out_shape=(big, line, line), in_specs=[anywhere] *...]
where the time goes in v3:
time: 78.2 us; the launch traced here: 78.1 us
  Pallas kernels  77.5 us (99%)
    pallas_call x1, Pallas kernels, body(): pl.pallas_call(kernel, out_shape=(big, line, line), in_specs=[anywhere] *...  76 us

profile of v3, /device:TPU:1, one launch (start us, length us, event | category | flops | bytes accessed | tf_op | source)
XLA Modules:
  0.0 78.1 jit_solution(11317808705151127467)
XLA Ops:
  0.6 76.0 %trajectory.1 = (f32[2048,128]{1,0:T(8,128)S(1)}, f32[1,128]{1,0:T(1,128)S(1)}, f32[1,128]{1,0:T(1,128)S(1)}) custom-call(f32[2048,128]{1,0:T(8,128)} %bitcast.3, f32[1,3,128,128]{3,2,1,0:T(8,128)} %gate_ref.1, s32[1,3,4,7]{3,2,1,0:T(4,128)} %bitcast.4, s32[4,3]{1,0:T(4,128)} %target_hbm.1), custom_call_target="tpu_custom_call" | custom-call | tf_op jit(solution)/shard_map/trajectory/pallas_call | solution.py:451
  76.6 1.5 %scale.1 = (f32[2048,128]{1,0:T(8,128)}, f32[1,4]{1,0:T(1,128)}) custom-call(f32[2048,128]{1,0:T(8,128)S(1)} %get-tuple-element.7.values_ref, f32[1,128]{1,0:T(1,128)S(1)} %get-tuple-element.8.scale_ref, f32[1,128]{1,0:T(1,128)S(1)} %get-tuple-element.9.logs_ref), custom_call_target="tpu_custom_call" | custom-call | tf_op jit(solution)/shard_map/scale/pallas_call | solution.py:473

commit v4 on v3

--- a/solution.py
+++ b/solution.py
@@ -52,19 +52,23 @@
 
 
 def block_transpose(arrays):
-    lane = lax.broadcasted_iota(jnp.int32, arrays[0].shape, 1)
-    low_half = lane < 64
-    even = (lane // 32) % 2 == 0
-    stage = [None] * 4
-    for a in range(2):
-        moved = pltpu.roll(jnp.where(low_half, arrays[a + 2], arrays[a]), 64, 1)
-        stage[a] = jnp.where(low_half, arrays[a], moved)
-        stage[a + 2] = jnp.where(low_half, moved, arrays[a + 2])
-    result = [None] * 4
-    for a in (0, 2):
-        result[a] = jnp.where(even, stage[a], pltpu.roll(stage[a + 1], 32, 1))
-        result[a + 1] = jnp.where(even, pltpu.roll(stage[a], 96, 1), stage[a + 1])
-    return result
+    block = lax.broadcasted_iota(jnp.int32, arrays[0].shape, 1) // 16
+    for bit in (4, 2, 1):
+        low = (block // bit) % 2 == 0
+        after = list(arrays)
+        for a in range(8):
+            if a & bit:
+                continue
+            here, there = arrays[a], arrays[a + bit]
+            if bit == 4:
+                moved = pltpu.roll(jnp.where(low, there, here), 64, 1)
+                after[a] = jnp.where(low, here, moved)
+                after[a + bit] = jnp.where(low, moved, there)
+            else:
+                after[a] = jnp.where(low, here, pltpu.roll(there, 16 * bit, 1))
+                after[a + bit] = jnp.where(low, pltpu.roll(here, REG - 16 * bit, 1), there)
+        arrays = after
+    return arrays
 
 
 def fold_squares(acc, x):
@@ -87,7 +91,7 @@
 def kernel(
     states_ref, gate_ref, kraus_hbm, target_hbm,
     y_ref, scale_ref, logs_ref,
-    kraus_ref, target_ref, x_ref, all_gates, send1, recv1, mid1, mid2, mid3, recv2, wide2, send3, recv3, h_mats, l_mats, sums_out, sums_in,
+    kraus_ref, target_ref, x_ref, all_gates, send1, recv1, mid1, mid2, mid3, quarters, recv2, wide2, send3, recv3, h_mats, l_mats, sums_out, sums_in,
     gate_send, gate_recv, pair_send, pair_recv,
     send1_sem, recv1_sem, send2_sem, recv2_sem, send3_sem, recv3_sem, sums_send, sums_recv,
     load_sems,
@@ -100,7 +104,7 @@
     j_me = (y_me % 2) * 2 + core
     m_me = (y_me // 2) * 8 + z_me
     slot_me = m_me * 4 + j_me
-    kappa_me = me // 4
+    kappa_me = me // 8
     partner = me + 1 - 2 * core
     zero = jnp.zeros((8, REG), F32)
 
@@ -136,14 +140,14 @@
     def to_all(send_one, flips=far_first):
         for flip_upper, flip_lower in flips:
             y = ((y_me // 2 + flip_upper) % 2) * 2 + (y_me + flip_lower) % 2
-            for on in (2, 1, 3, 0):
-                pair = (z_me // 2 + on) % 4
-
-                def one(n, carry, y=y, pair=pair):
-                    send_one(y, pair * 2 + (z_me + n // 2) % 2, (core + n) % 2)
+            for on in (1, 0):
+                half = (z_me // 4 + on) % 2
+
+                def one(n, carry, y=y, half=half):
+                    send_one(y, half * 4 + (z_me + n // 2) % 4, (core + n) % 2)
                     return carry
 
-                lax.fori_loop(0 if flip_upper or flip_lower or on else 1, 4, one, 0)
+                lax.fori_loop(0 if flip_upper or flip_lower or on else 1, 8, one, 0)
 
     width = 16
 
@@ -152,9 +156,9 @@
             m = k * width + i
             x = x_ref[pl.ds(m, REG, stride=MID), :]
             acc = fold_squares(acc, x)
-            pieces = block_transpose([x[q * 32 : (q + 1) * 32] for q in range(4)])
-            for j in range(4):
-                send1[part(m * 4 + j, 32), :] = pieces[j]
+            pieces = block_transpose([x[q * 16 : (q + 1) * 16] for q in range(8)])
+            for b in range(8):
+                send1[part(b % 2 * 64 + m * 4 + b // 2, 16), :] = pieces[b]
         return acc
 
     loads[0].wait()
@@ -164,10 +168,11 @@
 
     pl.semaphore_wait(barrier, PEERS - 1 + SECTIONS - 1)
 
-    def exchange(source, target, piece_of, slot, send_sem, recv_sem, group, flips):
+    def exchange(e, source, target, piece_of, slot, send_sem, recv_sem, group, flips):
         def one(y, z, c):
             pltpu.make_async_remote_copy(
-                source.at[part(piece_of(y, z, c), 32)], target.at[part(slot, 32)], send_sem, recv_sem.at[group],
+                source.at[part(e * 64 + piece_of(y, z, c), 16)], target.at[part(e * 64 + slot, 16)],
+                send_sem, recv_sem.at[group],
                 device_id=(seg, y * 16 + z * 2 + c), device_id_type=MESH,
             ).start()
 
@@ -179,8 +184,10 @@
     def piece_by_g(y, z, c):
         return y * 16 + z * 2 + c
 
-    exchange(send1, recv1, piece_by_m, me, send1_sem, recv1_sem, kappa_me, far_first)
-    recv1[part(me, 32), :] = send1[part(slot_me, 32), :]
+    for e in range(2):
+        exchange(e, send1, recv1, piece_by_m, me, send1_sem, recv1_sem, e * 8 + kappa_me, far_first)
+    for e in range(2):
+        recv1[part(e * 64 + me, 16), :] = send1[part(e * 64 + slot_me, 16), :]
 
     my_half = pl.ds(pl.multiple_of(core * 64, 64), 64)
     other_half = pl.ds(pl.multiple_of((1 - core) * 64, 64), 64)
@@ -229,7 +236,7 @@
     identity = (row == col).astype(F32)
     to_split = (col == (row % 64) * 2 + row // 64).astype(F32)
     from_split = (row == (col % 64) * 2 + col // 64).astype(F32)
-    to_lanes = (col == (row % 32 // 2) * 8 + (row // 32) * 2 + row % 2).astype(F32)
+    to_lanes = (col == (row % 16 // 2) * 16 + (row // 16) * 2 + row % 2).astype(F32)
 
     def noise(section, block):
         product = jnp.ones((REG, REG), F32)
@@ -273,82 +280,85 @@
             [ref[pl.ds(2 * index, rows, stride=stride), :], ref[pl.ds(2 * index + 1, rows, stride=stride), :]], axis=0
         )
 
-    def arrived(ref, sem, group, own):
-        @pl.when(group == own)
-        def _():
-            wait_bytes(ref, 3 * 32, sem.at[group])
-
-        @pl.when(group != own)
-        def _():
-            wait_bytes(ref, 4 * 32, sem.at[group])
-
-    def section0(k, carry):
-        flip, half = k // 2, k % 2
-        y = ((y_me // 2 + 1 - flip // 2) % 2) * 2 + (y_me + (flip + 1) // 2) % 2
-        kappas = [y * 4 + (z_me // 2 + 4 - on) % 4 for on in (2 + half, 1 - half)]
-        tall = []
-        for kappa in kappas:
-            arrived(recv1, recv1_sem, kappa, kappa_me)
-            parts = block_transpose([recv1[part(kappa * 4 + n, 32), :] for n in range(4)])
-            tall.append(jnp.concatenate(parts, axis=0))
-        wide = mix_rows(h_mats[0], jnp.concatenate(tall, axis=1))
-        for i, kappa in enumerate(kappas):
-            parts = block_transpose([wide[q * 32 : (q + 1) * 32, i * REG : (i + 1) * REG] for q in range(4)])
-            for n in range(4):
-                mid1[part(kappa * 4 + n, 32), :] = parts[n]
-        return carry
-
-    lax.fori_loop(0, 8, section0, 0)
-    step = 16
-
-    def section1(k, carry):
-        rs = [k * step + i for i in range(step)]
-        wide = mix_rows(h_mats[1], jnp.concatenate([split_rows(mid1, r, 32) for r in rs], axis=1))
-        for i, r in enumerate(rs):
-            parts = block_transpose([wide[n * 32 : (n + 1) * 32, i * REG : (i + 1) * REG] for n in range(4)])
-            for q in range(4):
-                mid2[part(q * 16 + r, 32), :] = parts[q]
-        return carry
-
-    lax.fori_loop(0, 16 // step, section1, 0)
-
-    def section2(k, carry):
-        kappas = [k * step + i for i in range(step)]
-        wide = mix_rows(h_mats[2], jnp.concatenate([split_rows(mid2, kappa, 32) for kappa in kappas], axis=1))
-        for i, kappa in enumerate(kappas):
-            parts = block_transpose([wide[q * 32 : (q + 1) * 32, i * REG : (i + 1) * REG] for q in range(4)])
-            for n in range(4):
-                mid3[part(kappa * 4 + n, 32), :] = parts[n]
-        return carry
-
-    lax.fori_loop(0, 16 // step, section2, 0)
-
-    mid2_tiles = mid2.reshape(64, 32, REG)
-    recv2_tiles = recv2.reshape(4, 64, 8, REG)
-
-    def send_quarter(k, carry):
-        j = (j_me + k) % 4
-        pltpu.make_async_remote_copy(
-            mid2_tiles.at[:, part(j, 8), :], recv2_tiles.at[j_me], send2_sem, recv2_sem,
-            device_id=(seg, (m_me // 8) * 32 + (j // 2) * 16 + z_me * 2 + j % 2), device_id_type=MESH,
-        ).start()
-        return carry
-
-    lax.fori_loop(1, 4, send_quarter, 0)
-
-    def section3(k, carry):
-        rs = [k * step + i for i in range(step)]
-        wide = mix_rows(h_mats[3], jnp.concatenate([split_rows(mid3, r, 32) for r in rs], axis=1))
-        for i, r in enumerate(rs):
-            here = wide[:, i * REG : (i + 1) * REG]
-            send3[pl.ds(2 * r, 64, stride=32), :] = here[:64]
-            send3[pl.ds(2 * r + 1, 64, stride=32), :] = here[64:]
-        return carry
-
-    lax.fori_loop(0, 16 // step, section3, 0)
-
-    exchange(send3, recv3, piece_by_g, slot_me, send3_sem, recv3_sem, m_me, near_first)
-    recv3[part(slot_me, 32), :] = send3[part(me, 32), :]
+    def arrived(ref, sem, group, own, pieces):
+        @pl.when(own)
+        def _():
+            wait_bytes(ref, (pieces - 1) * 16, sem.at[group])
+
+        @pl.when(jnp.logical_not(own))
+        def _():
+            wait_bytes(ref, pieces * 16, sem.at[group])
+
+    def chunk(wide, i, n):
+        return wide[n * 16 : (n + 1) * 16, i * REG : (i + 1) * REG]
+
+    def section0(e):
+        def some(k, carry):
+            y = ((y_me // 2 + 1 - k // 2) % 2) * 2 + (y_me + (k + 1) // 2) % 2
+            kappas = [y * 2 + (z_me // 4 + on) % 2 for on in (1, 0)]
+            tall = []
+            for kappa in kappas:
+                arrived(recv1, recv1_sem, e * 8 + kappa, kappa == kappa_me, 8)
+                parts = block_transpose([recv1[part(e * 64 + kappa * 8 + n, 16), :] for n in range(8)])
+                tall.append(jnp.concatenate(parts, axis=0))
+            wide = mix_rows(h_mats[0], jnp.concatenate(tall, axis=1))
+            for i, kappa in enumerate(kappas):
+                parts = block_transpose([chunk(wide, i, q) for q in range(8)])
+                for n in range(8):
+                    mid1[part(e * 64 + kappa * 8 + n, 16), :] = parts[n]
+            return carry
+
+        lax.fori_loop(0, 4, some, 0)
+
+    def half_rows(ref, e):
+        return ref.at[pl.ds(e * 1024, 1024)]
+
+    def section1(e):
+        source = half_rows(mid1, e)
+        wide = mix_rows(h_mats[1], jnp.concatenate([split_rows(source, r, 16) for r in range(8)], axis=1))
+        for r in range(8):
+            parts = block_transpose([chunk(wide, r, n) for n in range(8)])
+            for q in range(8):
+                mid2[part(e * 64 + q * 8 + r, 16), :] = parts[q]
+                for j in range(4):
+                    quarters[pl.ds(((j * 2 + e) * 64 + q * 8 + r) * 4, 4), :] = parts[q][j * 4 : (j + 1) * 4]
+
+    def section2(e):
+        source = half_rows(mid2, e)
+        wide = mix_rows(h_mats[2], jnp.concatenate([split_rows(source, kappa, 16) for kappa in range(8)], axis=1))
+        for kappa in range(8):
+            parts = block_transpose([chunk(wide, kappa, q) for q in range(8)])
+            for n in range(8):
+                mid3[part(e * 64 + kappa * 8 + n, 16), :] = parts[n]
+
+    def section3(e):
+        source = half_rows(mid3, e)
+        wide = mix_rows(h_mats[3], jnp.concatenate([split_rows(source, r, 16) for r in range(8)], axis=1))
+        target = half_rows(send3, e)
+        for r in range(8):
+            here = wide[:, r * REG : (r + 1) * REG]
+            target[pl.ds(2 * r, 64, stride=16), :] = here[:64]
+            target[pl.ds(2 * r + 1, 64, stride=16), :] = here[64:]
+
+    def send_quarters(e):
+        def one(k, carry):
+            j = (j_me + k) % 4
+            pltpu.make_async_remote_copy(
+                quarters.at[part(j * 2 + e, 256)], recv2.at[part(j_me * 2 + e, 256)], send2_sem, recv2_sem,
+                device_id=(seg, (m_me // 8) * 32 + (j // 2) * 16 + z_me * 2 + j % 2), device_id_type=MESH,
+            ).start()
+            return carry
+
+        lax.fori_loop(1, 4, one, 0)
+
+    for e in range(2):
+        section0(e)
+        section1(e)
+        section2(e)
+        send_quarters(e)
+        section3(e)
+        exchange(e, send3, recv3, piece_by_g, slot_me, send3_sem, recv3_sem, e * 16 + m_me, near_first)
+        recv3[part(e * 64 + slot_me, 16), :] = send3[part(e * 64 + me, 16), :]
 
     step = 4
 
@@ -360,19 +370,18 @@
 
     sum0 = lax.fori_loop(0, MID // step, norm0, zero)
     wait_bytes(recv2, 3 * 512, recv2_sem)
-    for n in range(4):
-        recv2_tiles[j_me, n * 16 : (n + 1) * 16] = mid2_tiles[n * 16 : (n + 1) * 16, part(j_me, 8), :]
+    recv2[part(j_me, 512), :] = quarters[part(j_me, 512), :]
 
     def norm1(k, acc):
-        parts = block_transpose([recv2[part(j * 4 + k, REG), :] for j in range(4)])
-        for y in range(4):
-            wide2[part(y * 4 + k, REG), :] = parts[y]
+        parts = block_transpose([recv2[pl.ds(pl.multiple_of(b * 256 + k * 64, 64), 64), :] for b in range(8)])
+        for n in range(8):
+            wide2[pl.ds(pl.multiple_of(n * 256 + k * 64, 64), 64), :] = parts[n]
         return fold_squares(acc, mix_lanes(jnp.concatenate(parts, axis=0), l_mats[1]))
 
     sum1 = lax.fori_loop(0, 4, norm1, zero)
 
     def norm2(k, acc):
-        xs = [split_rows(wide2.at[part(k, 512)], i, 8) for i in range(4)]
+        xs = [split_rows(wide2.at[part(2 * k + i // 2, 256)], i % 2, 4) for i in range(4)]
         wide = mix_rows(h_mats[2], jnp.concatenate(xs, axis=1))
         tall = jnp.concatenate([wide[:, i * REG : (i + 1) * REG] for i in range(4)], axis=0)
         return fold_squares(acc, mix_lanes(tall, l_mats[2]))
@@ -380,14 +389,14 @@
     sum2 = lax.fori_loop(0, 4, norm2, zero)
 
     def last(k, acc):
-        on = k % 4
-        pair = (z_me // 2 + jnp.where(on < 2, on + 2, 3 - on)) % 4
         upper = (y_me // 2 + k // 4) % 2
-        ms = [upper * 8 + pair * 2, upper * 8 + pair * 2 + 1]
+        z = ((z_me // 4 + 1 - k % 4 // 2) % 2) * 4 + 2 * (k % 2)
+        ms = [upper * 8 + z, upper * 8 + z + 1]
         tall = []
         for m in ms:
-            arrived(recv3, recv3_sem, m, m_me)
-            tall += block_transpose([recv3[part(m * 4 + j, 32), :] for j in range(4)])
+            for e in range(2):
+                arrived(recv3, recv3_sem, e * 16 + m, m == m_me, 4)
+            tall += block_transpose([recv3[part(b % 2 * 64 + m * 4 + b // 2, 16), :] for b in range(8)])
         mixed = mix_lanes(jnp.concatenate(tall, axis=0), l_mats[3])
         for i, m in enumerate(ms):
             y_ref[pl.ds(m, REG, stride=MID), :] = mixed[i * REG : (i + 1) * REG]
@@ -419,9 +428,9 @@
         def _():
             pair_copy(section).wait_send()
 
-    wait_bytes(send1, 63 * 32, send1_sem)
+    wait_bytes(send1, 126 * 16, send1_sem)
     wait_bytes(recv2, 3 * 512, send2_sem)
-    wait_bytes(send3, 63 * 32, send3_sem)
+    wait_bytes(send3, 126 * 16, send3_sem)
     wait_bytes(sums_in, 63, sums_send)
     wait_bytes(sums_in, 63, sums_recv)
     totals = jnp.sum(sums_in[...], axis=0)
@@ -458,13 +467,13 @@
             pltpu.SMEM((SECTIONS, BLOCKS), jnp.int32),
             big,
             pltpu.VMEM((SECTIONS, BLOCKS, REG, REG), F32),
-            big, big, big, big, big, big, big, big, big,
+            big, big, big, big, big, big, big, big, big, big,
             pltpu.VMEM((SECTIONS, REG, 3 * REG), BF16),
             pltpu.VMEM((SECTIONS, 3 * REG, REG), BF16),
             pltpu.VMEM((1, REG), F32),
             pltpu.VMEM((PEERS, 1, REG), F32),
             dma((SECTIONS,)), dma((SECTIONS,)), dma((SECTIONS,)), dma((SECTIONS,)),
-            dma, dma((16,)), dma, dma, dma, dma((16,)), dma, dma,
+            dma, dma((16,)), dma, dma, dma, dma((32,)), dma, dma,
             dma((4,)),
         ],
         compiler_params=pltpu.CompilerParams(collective_id=0, has_side_effects=True),

time: 78.2 us -> 71.6 us (0.916)
  Pallas kernels: 77.5 us -> 70.8 us
    pallas_call x1, Pallas kernels: 76 us -> 69.3 us  [body(): pl.pallas_call(kernel, out_shape=(big, line, line), in_specs=[anywhere] *...]
where the time goes in v4:
time: 71.6 us; the launch traced here: 71.4 us
  Pallas kernels  70.8 us (99%)
    pallas_call x1, Pallas kernels, body(): pl.pallas_call(kernel, out_shape=(big, line, line), in_specs=[anywhere] *...  69.3 us
    pallas_call x1, Pallas kernels, body(): pl.pallas_call(scale_kernel, out_shape=(jax.ShapeDtypeStruct((ROWS, REG),...  1.53 us

profile of v4, /device:TPU:1, one launch (start us, length us, event | category | flops | bytes accessed | tf_op | source)
XLA Modules:
  0.0 71.4 jit_solution(688356159768649748)
XLA Ops:
  0.6 69.3 %trajectory.1 = (f32[2048,128]{1,0:T(8,128)S(1)}, f32[1,128]{1,0:T(1,128)S(1)}, f32[1,128]{1,0:T(1,128)S(1)}) custom-call(f32[2048,128]{1,0:T(8,128)} %bitcast.3, f32[1,3,128,128]{3,2,1,0:T(8,128)} %gate_ref.1, s32[1,3,4,7]{3,2,1,0:T(4,128)} %bitcast.4, s32[4,3]{1,0:T(4,128)} %target_hbm.1), custom_call_target="tpu_custom_call" | custom-call | tf_op jit(solution)/shard_map/trajectory/pallas_call | solution.py:460
  69.9 1.5 %scale.1 = (f32[2048,128]{1,0:T(8,128)}, f32[1,4]{1,0:T(1,128)}) custom-call(f32[2048,128]{1,0:T(8,128)S(1)} %get-tuple-element.7.values_ref, f32[1,128]{1,0:T(1,128)S(1)} %get-tuple-element.8.scale_ref, f32[1,128]{1,0:T(1,128)S(1)} %get-tuple-element.9.logs_ref), custom_call_target="tpu_custom_call" | custom-call | tf_op jit(solution)/shard_map/scale/pallas_call | solution.py:482

commit v5 on v4

--- a/solution.py
+++ b/solution.py
@@ -91,7 +91,7 @@
 def kernel(
     states_ref, gate_ref, kraus_hbm, target_hbm,
     y_ref, scale_ref, logs_ref,
-    kraus_ref, target_ref, x_ref, all_gates, send1, recv1, mid1, mid2, mid3, quarters, recv2, wide2, send3, recv3, h_mats, l_mats, sums_out, sums_in,
+    kraus_ref, target_ref, x_ref, all_gates, send1, recv1, mid1, mid2, mid3, quarters, recv2, wide2, send3, recv3, h_mats, l_mats, noises, lows, sums_out, sums_in,
     gate_send, gate_recv, pair_send, pair_recv,
     send1_sem, recv1_sem, send2_sem, recv2_sem, send3_sem, recv3_sem, sums_send, sums_recv,
     load_sems,
@@ -184,11 +184,6 @@
     def piece_by_g(y, z, c):
         return y * 16 + z * 2 + c
 
-    for e in range(2):
-        exchange(e, send1, recv1, piece_by_m, me, send1_sem, recv1_sem, e * 8 + kappa_me, far_first)
-    for e in range(2):
-        recv1[part(e * 64 + me, 16), :] = send1[part(e * 64 + slot_me, 16), :]
-
     my_half = pl.ds(pl.multiple_of(core * 64, 64), 64)
     other_half = pl.ds(pl.multiple_of((1 - core) * 64, 64), 64)
 
@@ -255,15 +250,22 @@
                 mixed = gate
             else:
                 mixed = exact_dot(gate, jnp.where(on_low, low, high))
-            mixed = noise(section, block) * mixed
+            mixed = noises[section, block] * mixed
             low, high = jnp.where(on_low, mixed, low), jnp.where(on_low, high, mixed)
         return low, high
 
     for section in range(SECTIONS):
         send_gates(section)
+    for e in range(2):
+        exchange(e, send1, recv1, piece_by_m, me, send1_sem, recv1_sem, e * 8 + kappa_me, far_first)
+    for e in range(2):
+        recv1[part(e * 64 + me, 16), :] = send1[part(e * 64 + slot_me, 16), :]
+
+    for section in range(SECTIONS):
+        for block in range(BLOCKS):
+            noises[section, block] = noise(section, block)
     for section in range(SECTIONS):
         pass_gates(section)
-    low_all = None
     for section in range(SECTIONS):
         end_gates(section)
         low, high = compose(section)
@@ -272,8 +274,7 @@
         if section % 2 == 1:
             high = exact_dot(to_lanes if section == 1 else to_split, high)
         h_mats[section] = rows_cat(high)
-        low_all = low if section == 0 else exact_dot(low, low_all)
-        l_mats[section] = lanes_cat(low_all.T)
+        lows[section] = low
 
     def split_rows(ref, index, stride, rows=64):
         return jnp.concatenate(
@@ -293,12 +294,15 @@
         return wide[n * 16 : (n + 1) * 16, i * REG : (i + 1) * REG]
 
     def section0(e):
-        def some(k, carry):
-            y = ((y_me // 2 + 1 - k // 2) % 2) * 2 + (y_me + (k + 1) // 2) % 2
-            kappas = [y * 2 + (z_me // 4 + on) % 2 for on in (1, 0)]
+        def some(steps):
+            kappas = []
+            for k in steps:
+                y = ((y_me // 2 + 1 - k // 2) % 2) * 2 + (y_me + (k + 1) // 2) % 2
+                kappas += [y * 2 + (z_me // 4 + on) % 2 for on in (1, 0)]
             tall = []
             for kappa in kappas:
                 arrived(recv1, recv1_sem, e * 8 + kappa, kappa == kappa_me, 8)
+            for kappa in kappas:
                 parts = block_transpose([recv1[part(e * 64 + kappa * 8 + n, 16), :] for n in range(8)])
                 tall.append(jnp.concatenate(parts, axis=0))
             wide = mix_rows(h_mats[0], jnp.concatenate(tall, axis=1))
@@ -306,9 +310,9 @@
                 parts = block_transpose([chunk(wide, i, q) for q in range(8)])
                 for n in range(8):
                     mid1[part(e * 64 + kappa * 8 + n, 16), :] = parts[n]
-            return carry
-
-        lax.fori_loop(0, 4, some, 0)
+
+        for steps in ((0, 1, 2, 3),) if e == 0 else ((0, 1), (2, 3)):
+            some(steps)
 
     def half_rows(ref, e):
         return ref.at[pl.ds(e * 1024, 1024)]
@@ -359,6 +363,12 @@
         section3(e)
         exchange(e, send3, recv3, piece_by_g, slot_me, send3_sem, recv3_sem, e * 16 + m_me, near_first)
         recv3[part(e * 64 + slot_me, 16), :] = send3[part(e * 64 + me, 16), :]
+
+    low_all = lows[0]
+    l_mats[0] = lanes_cat(low_all.T)
+    for section in range(1, SECTIONS):
+        low_all = exact_dot(lows[section], low_all)
+        l_mats[section] = lanes_cat(low_all.T)
 
     step = 4
 
@@ -439,16 +449,18 @@
     scale_ref[...] = 1.0 / jnp.sqrt(jnp.full((1, REG), mean, F32))
 
 
-def scale_kernel(values_ref, scale_ref, logs_ref, y_ref, log_weights_ref, scaled, sems):
-    log_weights_ref[...] = logs_ref[:, :SECTIONS]
+def scale_kernel(values_ref, scale_ref, logs_ref, y_ref, log_weights_ref, scaled, logs, sems):
+    logs[...] = logs_ref[:, :SECTIONS]
     rows = ROWS // 4
+    copies = [pltpu.make_async_copy(logs, log_weights_ref, sems.at[4])]
     for n in range(4):
         part = pl.ds(n * rows, rows)
         scaled[part, :] = values_ref[part, :] * scale_ref[...]
-        pltpu.make_async_copy(scaled.at[part], y_ref.at[part], sems.at[n]).start()
-    for n in range(4):
-        part = pl.ds(n * rows, rows)
-        pltpu.make_async_copy(scaled.at[part], y_ref.at[part], sems.at[n]).wait()
+        copies.append(pltpu.make_async_copy(scaled.at[part], y_ref.at[part], sems.at[n]))
+        copies[-1].start()
+    copies[0].start()
+    for copy in copies:
+        copy.wait()
 
 
 def body(states, gate_blocks, kraus_picks, block_targets):
@@ -470,6 +482,8 @@
             big, big, big, big, big, big, big, big, big, big,
             pltpu.VMEM((SECTIONS, REG, 3 * REG), BF16),
             pltpu.VMEM((SECTIONS, 3 * REG, REG), BF16),
+            pltpu.VMEM((SECTIONS, BLOCKS, REG, REG), F32),
+            pltpu.VMEM((SECTIONS, REG, REG), F32),
             pltpu.VMEM((1, REG), F32),
             pltpu.VMEM((PEERS, 1, REG), F32),
             dma((SECTIONS,)), dma((SECTIONS,)), dma((SECTIONS,)), dma((SECTIONS,)),
@@ -483,8 +497,8 @@
         scale_kernel,
         out_shape=(jax.ShapeDtypeStruct((ROWS, REG), F32), jax.ShapeDtypeStruct((1, SECTIONS), F32)),
         in_specs=[vmem, vmem, vmem],
-        out_specs=(anywhere, vmem),
-        scratch_shapes=[big, dma((4,))],
+        out_specs=(anywhere, anywhere),
+        scratch_shapes=[big, pltpu.VMEM((1, SECTIONS), F32), dma((5,))],
         compiler_params=pltpu.CompilerParams(vmem_limit_bytes=8 * 2**20),
         name="scale",
     )(values, scale, logs)

time: 71.6 us -> 71.2 us (level)
  no operation moved by 1% of the time
where the time goes in v5:
time: 71.2 us; the launch traced here: 71.1 us
  Pallas kernels  70.4 us (99%)
    pallas_call x1, Pallas kernels, body(): pl.pallas_call(kernel, out_shape=(big, line, line), in_specs=[anywhere] *...  69.4 us

profile of v5, /device:TPU:1, one launch (start us, length us, event | category | flops | bytes accessed | tf_op | source)
XLA Modules:
  0.0 71.1 jit_solution(1010113535849652852)
XLA Ops:
  0.6 69.4 %trajectory.1 = (f32[2048,128]{1,0:T(8,128)S(1)}, f32[1,128]{1,0:T(1,128)S(1)}, f32[1,128]{1,0:T(1,128)S(1)}) custom-call(f32[2048,128]{1,0:T(8,128)} %bitcast.3, f32[1,3,128,128]{3,2,1,0:T(8,128)} %gate_ref.1, s32[1,3,4,7]{3,2,1,0:T(4,128)} %bitcast.4, s32[4,3]{1,0:T(4,128)} %target_hbm.1), custom_call_target="tpu_custom_call" | custom-call | tf_op jit(solution)/shard_map/trajectory/pallas_call | solution.py:472
  70.0 1.0 %scale.1 = (f32[2048,128]{1,0:T(8,128)}, f32[1,4]{1,0:T(1,128)}) custom-call(f32[2048,128]{1,0:T(8,128)S(1)} %get-tuple-element.7.values_ref, f32[1,128]{1,0:T(1,128)S(1)} %get-tuple-element.8.scale_ref, f32[1,128]{1,0:T(1,128)S(1)} %get-tuple-element.9.logs_ref), custom_call_target="tpu_custom_call" | custom-call | tf_op jit(solution)/shard_map/scale/pallas_call | solution.py:496

commit v6 on v5

--- a/solution.py
+++ b/solution.py
@@ -134,20 +134,20 @@
     for k in range(1, SECTIONS):
         pl.semaphore_signal(barrier, inc=1, device_id=((seg + k) % SECTIONS, me), device_id_type=MESH)
 
-    far_first = ((1, 0), (1, 1), (0, 1), (0, 0))
-    near_first = far_first[::-1]
-
-    def to_all(send_one, flips=far_first):
-        for flip_upper, flip_lower in flips:
-            y = ((y_me // 2 + flip_upper) % 2) * 2 + (y_me + flip_lower) % 2
-            for on in (1, 0):
-                half = (z_me // 4 + on) % 2
-
-                def one(n, carry, y=y, half=half):
-                    send_one(y, half * 4 + (z_me + n // 2) % 4, (core + n) % 2)
-                    return carry
-
-                lax.fori_loop(0 if flip_upper or flip_lower or on else 1, 8, one, 0)
+    y_far_first = ((1, 0, 1), (1, 0, 0), (1, 1, 1), (1, 1, 0), (0, 1, 1), (0, 1, 0), (0, 0, 1), (0, 0, 0))
+    y_near_first = ((0, 0, 1), (0, 0, 0), (0, 1, 1), (0, 1, 0), (1, 1, 1), (1, 1, 0), (1, 0, 1), (1, 0, 0))
+    last_order = ((0, 1), (0, 0), (1, 1), (1, 0))
+
+    def to_all(send_one, flips=y_far_first):
+        for flip in flips:
+            y = ((y_me // 2 + flip[0]) % 2) * 2 + (y_me + flip[1]) % 2
+            half = (z_me // 4 + flip[2]) % 2
+
+            def one(n, carry, y=y, half=half):
+                send_one(y, half * 4 + (z_me + n // 2) % 4, (core + n) % 2)
+                return carry
+
+            lax.fori_loop(0 if any(flip) else 1, 8, one, 0)
 
     width = 16
 
@@ -257,7 +257,7 @@
     for section in range(SECTIONS):
         send_gates(section)
     for e in range(2):
-        exchange(e, send1, recv1, piece_by_m, me, send1_sem, recv1_sem, e * 8 + kappa_me, far_first)
+        exchange(e, send1, recv1, piece_by_m, me, send1_sem, recv1_sem, e * 8 + kappa_me, y_far_first)
     for e in range(2):
         recv1[part(e * 64 + me, 16), :] = send1[part(e * 64 + slot_me, 16), :]
 
@@ -361,7 +361,7 @@
         section2(e)
         send_quarters(e)
         section3(e)
-        exchange(e, send3, recv3, piece_by_g, slot_me, send3_sem, recv3_sem, e * 16 + m_me, near_first)
+        exchange(e, send3, recv3, piece_by_g, slot_me, send3_sem, recv3_sem, e * 16 + m_me, y_near_first)
         recv3[part(e * 64 + slot_me, 16), :] = send3[part(e * 64 + me, 16), :]
 
     low_all = lows[0]
@@ -398,10 +398,8 @@
 
     sum2 = lax.fori_loop(0, 4, norm2, zero)
 
-    def last(k, acc):
-        upper = (y_me // 2 + k // 4) % 2
-        z = ((z_me // 4 + 1 - k % 4 // 2) % 2) * 4 + 2 * (k % 2)
-        ms = [upper * 8 + z, upper * 8 + z + 1]
+    def last(upper, half, count, k, acc):
+        ms = [upper * 8 + half * 4 + k * count + i for i in range(count)]
         tall = []
         for m in ms:
             for e in range(2):
@@ -412,7 +410,12 @@
             y_ref[pl.ds(m, REG, stride=MID), :] = mixed[i * REG : (i + 1) * REG]
         return fold_squares(acc, mixed)
 
-    sum3 = lax.fori_loop(0, 8, last, zero)
+    sum3 = zero
+    for flip_upper, flip_half in last_order:
+        upper = (y_me // 2 + flip_upper) % 2
+        half = (z_me // 4 + flip_half) % 2
+        count = 1 if (flip_upper, flip_half) == last_order[-1] else 2
+        sum3 = lax.fori_loop(0, 4 // count, functools.partial(last, upper, half, count), sum3)
 
     lane = lax.broadcasted_iota(jnp.int32, (1, REG), 1)
     line = jnp.ones((1, REG), F32)

time: 71.2 us -> 71.3 us (level)
  no operation moved by 1% of the time
where the time goes in v6:
time: 71.3 us; the launch traced here: 71.2 us
  Pallas kernels  70.6 us (99%)
    pallas_call x1, Pallas kernels, body(): pl.pallas_call(kernel, out_shape=(big, line, line), in_specs=[anywhere] *...  69.5 us

profile of v6, /device:TPU:1, one launch (start us, length us, event | category | flops | bytes accessed | tf_op | source)
XLA Modules:
  0.0 71.2 jit_solution(6706375360275177689)
XLA Ops:
  0.6 69.5 %trajectory.1 = (f32[2048,128]{1,0:T(8,128)S(1)}, f32[1,128]{1,0:T(1,128)S(1)}, f32[1,128]{1,0:T(1,128)S(1)}) custom-call(f32[2048,128]{1,0:T(8,128)} %bitcast.3, f32[1,3,128,128]{3,2,1,0:T(8,128)} %gate_ref.1, s32[1,3,4,7]{3,2,1,0:T(4,128)} %bitcast.4, s32[4,3]{1,0:T(4,128)} %target_hbm.1), custom_call_target="tpu_custom_call" | custom-call | tf_op jit(solution)/shard_map/trajectory/pallas_call | solution.py:475
  70.2 1.0 %scale.1 = (f32[2048,128]{1,0:T(8,128)}, f32[1,4]{1,0:T(1,128)}) custom-call(f32[2048,128]{1,0:T(8,128)S(1)} %get-tuple-element.7.values_ref, f32[1,128]{1,0:T(1,128)S(1)} %get-tuple-element.8.scale_ref, f32[1,128]{1,0:T(1,128)S(1)} %get-tuple-element.9.logs_ref), custom_call_target="tpu_custom_call" | custom-call | tf_op jit(solution)/shard_map/scale/pallas_call | solution.py:499

commit v7 on v5

--- a/solution.py
+++ b/solution.py
@@ -129,8 +129,8 @@
         pl.semaphore_signal(barrier, inc=1, device_id=(seg, (me + k) % PEERS), device_id_type=MESH)
         return carry
 
-    lax.fori_loop(40, PEERS, greet, 0)
-    lax.fori_loop(1, 40, greet, 0)
+    lax.fori_loop(34, PEERS, greet, 0)
+    lax.fori_loop(1, 34, greet, 0)
     for k in range(1, SECTIONS):
         pl.semaphore_signal(barrier, inc=1, device_id=((seg + k) % SECTIONS, me), device_id_type=MESH)
 
@@ -398,6 +398,25 @@
 
     sum2 = lax.fori_loop(0, 4, norm2, zero)
 
+    for section in range(SECTIONS):
+        @pl.when(seg == section)
+        def _():
+            for k in range(1, SECTIONS):
+                gate_copy(section, (seg + k) % SECTIONS).wait_send()
+
+        @pl.when(seg != section)
+        def _():
+            pair_copy(section).wait_send()
+
+    wait_bytes(send1, 126 * 16, send1_sem)
+    wait_bytes(recv2, 3 * 512, send2_sem)
+
+    lane = lax.broadcasted_iota(jnp.int32, (1, REG), 1)
+    known = jnp.ones((1, REG), F32)
+    for n, acc in enumerate((first_sum, sum0, sum1, sum2)):
+        known = jnp.where(lane == n, jnp.sum(acc), known)
+    sums_out[...] = known
+
     def last(k, acc):
         upper = (y_me // 2 + k // 4) % 2
         z = ((z_me // 4 + 1 - k % 4 // 2) % 2) * 4 + 2 * (k % 2)
@@ -414,10 +433,7 @@
 
     sum3 = lax.fori_loop(0, 8, last, zero)
 
-    lane = lax.broadcasted_iota(jnp.int32, (1, REG), 1)
-    line = jnp.ones((1, REG), F32)
-    for n, acc in enumerate((first_sum, sum0, sum1, sum2, sum3)):
-        line = jnp.where(lane == n, jnp.sum(acc), line)
+    line = jnp.where(lane == 4, jnp.sum(sum3), sums_out[...])
     sums_out[...] = line
     sums_in[me] = line
 
@@ -428,18 +444,6 @@
 
     to_all(send_sums)
 
-    for section in range(SECTIONS):
-        @pl.when(seg == section)
-        def _():
-            for k in range(1, SECTIONS):
-                gate_copy(section, (seg + k) % SECTIONS).wait_send()
-
-        @pl.when(seg != section)
-        def _():
-            pair_copy(section).wait_send()
-
-    wait_bytes(send1, 126 * 16, send1_sem)
-    wait_bytes(recv2, 3 * 512, send2_sem)
     wait_bytes(send3, 126 * 16, send3_sem)
     wait_bytes(sums_in, 63, sums_send)
     wait_bytes(sums_in, 63, sums_recv)

time: 71.2 us -> 71.4 us (level)
  no operation moved by 1% of the time
where the time goes in v7:
time: 71.4 us; the launch traced here: 71.3 us
  Pallas kernels  70.7 us (99%)
    pallas_call x1, Pallas kernels, body(): pl.pallas_call(kernel, out_shape=(big, line, line), in_specs=[anywhere] *...  69.7 us

profile of v7, /device:TPU:1, one launch (start us, length us, event | category | flops | bytes accessed | tf_op | source)
XLA Modules:
  0.0 71.3 jit_solution(9872335968255545103)
XLA Ops:
  0.6 69.7 %trajectory.1 = (f32[2048,128]{1,0:T(8,128)S(1)}, f32[1,128]{1,0:T(1,128)S(1)}, f32[1,128]{1,0:T(1,128)S(1)}) custom-call(f32[2048,128]{1,0:T(8,128)} %bitcast.3, f32[1,3,128,128]{3,2,1,0:T(8,128)} %gate_ref.1, s32[1,3,4,7]{3,2,1,0:T(4,128)} %bitcast.4, s32[4,3]{1,0:T(4,128)} %target_hbm.1), custom_call_target="tpu_custom_call" | custom-call | tf_op jit(solution)/shard_map/trajectory/pallas_call | solution.py:476
  70.3 1.0 %scale.1 = (f32[2048,128]{1,0:T(8,128)}, f32[1,4]{1,0:T(1,128)}) custom-call(f32[2048,128]{1,0:T(8,128)S(1)} %get-tuple-element.7.values_ref, f32[1,128]{1,0:T(1,128)S(1)} %get-tuple-element.8.scale_ref, f32[1,128]{1,0:T(1,128)S(1)} %get-tuple-element.9.logs_ref), custom_call_target="tpu_custom_call" | custom-call | tf_op jit(solution)/shard_map/scale/pallas_call | solution.py:500

commit v8 on v5

--- a/solution.py
+++ b/solution.py
@@ -451,9 +451,9 @@
 
 def scale_kernel(values_ref, scale_ref, logs_ref, y_ref, log_weights_ref, scaled, logs, sems):
     logs[...] = logs_ref[:, :SECTIONS]
-    rows = ROWS // 4
-    copies = [pltpu.make_async_copy(logs, log_weights_ref, sems.at[4])]
-    for n in range(4):
+    rows = ROWS // 8
+    copies = [pltpu.make_async_copy(logs, log_weights_ref, sems.at[8])]
+    for n in range(8):
         part = pl.ds(n * rows, rows)
         scaled[part, :] = values_ref[part, :] * scale_ref[...]
         copies.append(pltpu.make_async_copy(scaled.at[part], y_ref.at[part], sems.at[n]))
@@ -498,7 +498,7 @@
         out_shape=(jax.ShapeDtypeStruct((ROWS, REG), F32), jax.ShapeDtypeStruct((1, SECTIONS), F32)),
         in_specs=[vmem, vmem, vmem],
         out_specs=(anywhere, anywhere),
-        scratch_shapes=[big, pltpu.VMEM((1, SECTIONS), F32), dma((5,))],
+        scratch_shapes=[big, pltpu.VMEM((1, SECTIONS), F32), dma((9,))],
         compiler_params=pltpu.CompilerParams(vmem_limit_bytes=8 * 2**20),
         name="scale",
     )(values, scale, logs)

time: 71.2 us -> 71.2 us (level)
  no operation moved by 1% of the time
where the time goes in v8:
time: 71.2 us; the launch traced here: 71.1 us
  Pallas kernels  70.5 us (99%)
    pallas_call x1, Pallas kernels, body(): pl.pallas_call(kernel, out_shape=(big, line, line), in_specs=[anywhere] *...  69.4 us

profile of v8, /device:TPU:1, one launch (start us, length us, event | category | flops | bytes accessed | tf_op | source)
XLA Modules:
  0.0 71.1 jit_solution(13709867020691832744)
XLA Ops:
  0.6 69.4 %trajectory.1 = (f32[2048,128]{1,0:T(8,128)S(1)}, f32[1,128]{1,0:T(1,128)S(1)}, f32[1,128]{1,0:T(1,128)S(1)}) custom-call(f32[2048,128]{1,0:T(8,128)} %bitcast.3, f32[1,3,128,128]{3,2,1,0:T(8,128)} %gate_ref.1, s32[1,3,4,7]{3,2,1,0:T(4,128)} %bitcast.4, s32[4,3]{1,0:T(4,128)} %target_hbm.1), custom_call_target="tpu_custom_call" | custom-call | tf_op jit(solution)/shard_map/trajectory/pallas_call | solution.py:472
  70.0 1.0 %scale.1 = (f32[2048,128]{1,0:T(8,128)}, f32[1,4]{1,0:T(1,128)}) custom-call(f32[2048,128]{1,0:T(8,128)S(1)} %get-tuple-element.7.values_ref, f32[1,128]{1,0:T(1,128)S(1)} %get-tuple-element.8.scale_ref, f32[1,128]{1,0:T(1,128)S(1)} %get-tuple-element.9.logs_ref), custom_call_target="tpu_custom_call" | custom-call | tf_op jit(solution)/shard_map/scale/pallas_call | solution.py:496
